TPU v7x, 32 devices: a whole 2x2x4 slice. The times are simulated.
32 devices in a mesh: seq: 8 (over y, x, core), batch: 4 (over z).
Axes of the slice: x: 2, y: 2, z: 4, core: 2. Of those that a mesh axis runs over, the one named last changes fastest.
Arguments:
- tokens: bfloat16 [4, 1024, 1024], P('batch', 'seq'), may hold values from -6 to 6
- out_grad: bfloat16 [4, 1024, 1024], P('batch', 'seq'), may hold values from -6 to 6
- group_id: int32 [4], P('batch'), may hold values from 0 to 7
- group_weight: float32 [8], replicated, may hold values from 0.25 to 4
- gain_attn: float32 [1024], P(('seq', 'batch')), may hold values from 0.5 to 1.5
- w_query: float32 [1024, 1024], P(('seq', 'batch')), may hold values from -0.1875 to 0.1875
- w_qrope: float32 [1024, 1024], P(('seq', 'batch')), may hold values from -0.1875 to 0.1875
- w_latent: float32 [1024, 512], P(('seq', 'batch')), may hold values from -0.1875 to 0.1875
- w_krope: float32 [1024, 64], P(('seq', 'batch')), may hold values from -0.1875 to 0.1875
- w_ukey: float32 [1024, 256], P(('seq', 'batch')), may hold values from -0.75 to 0.75
- w_uval: float32 [1024, 256], P(('seq', 'batch')), may hold values from -0.375 to 0.375
- w_out: float32 [1024, 1024], P(('seq', 'batch')), may hold values from -1.5 to 1.5
- gain_ffn: float32 [1024], P(('seq', 'batch')), may hold values from 0.5 to 1.5
- w_gate: float32 [1024, 2816], P(('seq', 'batch')), may hold values from -0.1875 to 0.1875
- w_up: float32 [1024, 2816], P(('seq', 'batch')), may hold values from -0.1875 to 0.1875
- w_down: float32 [2816, 1024], P(('seq', 'batch')), may hold values from -0.109375 to 0.109375
Outputs:
- block_out: bfloat16 [4, 1024, 1024], P('batch', 'seq')
- tokens_grad: float32 [4, 1024, 1024], P('batch', 'seq')
- gain_attn_grad: float32 [1024], P(('seq', 'batch'))
- w_query_grad: float32 [1024, 1024], P(('seq', 'batch'))
- w_qrope_grad: float32 [1024, 1024], P(('seq', 'batch'))
- w_latent_grad: float32 [1024, 512], P(('seq', 'batch'))
- w_krope_grad: float32 [1024, 64], P(('seq', 'batch'))
- w_ukey_grad: float32 [1024, 256], P(('seq', 'batch'))
- w_uval_grad: float32 [1024, 256], P(('seq', 'batch'))
- w_out_grad: float32 [1024, 1024], P(('seq', 'batch'))
- gain_ffn_grad: float32 [1024], P(('seq', 'batch'))
- w_gate_grad: float32 [1024, 2816], P(('seq', 'batch'))
- w_up_grad: float32 [1024, 2816], P(('seq', 'batch'))
- w_down_grad: float32 [2816, 1024], P(('seq', 'batch'))
Inputs may be any that keep to these rules, and one draw needn't show every extreme that they name: `group_id`: each sequence's domain group, an index into group_weight.
All inputs are finite; a program needn't handle non-finite values.
Results may differ from a plain program's by a relative error of at most 0.02.
Values may be sent and summed in bfloat16 or wider, within the bound.
A program may use at most 256 MiB of HBM per device.

v0:
```python
import jax
import jax.numpy as jnp
from jax import lax
from jax.sharding import PartitionSpec as P

FF = 2816
H = 16
HD = 64
GROUPS = 2
LAT = 256
ROPE = 64


EPSILON = 1e-05
ROTARY_BASE = 10000.0
NEG_FILL = -1e30


def from_behind(x, axis, by):
    devices = lax.axis_size(axis)
    return lax.ppermute(x, axis, [(i, (i + by) % devices) for i in range(devices)])


def from_behind_2(x, axis, by):
    devices = lax.axis_size(axis)
    pairs = [(i, i + by) for i in range(devices) if 0 <= i + by < devices]
    return lax.ppermute(x, axis, pairs)


def matmul(left_side, right_side):
    return jnp.dot(left_side, right_side, preferred_element_type=jnp.float32)


def left_inner(left_side, right_side):
    return lax.dot_general(
        left_side, right_side, (((0,), (0,)), ((), ())), preferred_element_type=jnp.float32
    )


def right_inner(left_side, right_side):
    return lax.dot_general(
        left_side, right_side, (((1,), (1,)), ((), ())), preferred_element_type=jnp.float32
    )


def norm_apply(values, norm_gain):
    inverse = lax.rsqrt(jnp.mean(values * values, -1, keepdims=True) + EPSILON)
    return (inverse, values * inverse * norm_gain)


def norm_grad(values, inverse, norm_gain, incoming):
    scaled = incoming * norm_gain
    back_part = inverse * scaled - values * (inverse * inverse * inverse) * jnp.mean(
        scaled * values, -1, keepdims=True
    )
    return (back_part, jnp.sum(incoming * values * inverse, 0))


def rotate(values, position, direction):
    half_width = values.shape[-1] // 2
    frequency = ROTARY_BASE ** (
        -jnp.arange(half_width).astype(jnp.float32) * 2.0 / values.shape[-1]
    )
    angles = position[..., None, None] * frequency
    cosine = jnp.cos(angles)
    sine_part = direction * jnp.sin(angles)
    first_half = values[..., :half_width]
    second_half = values[..., half_width:]
    return jnp.concatenate(
        [
            first_half * cosine - second_half * sine_part,
            first_half * sine_part + second_half * cosine,
        ],
        -1,
    )


def block_scores(query_latent, query_rope, key_latent, key_rope, scaling, diagonal):
    scores = jnp.einsum(
        "sqgpf,skgf->sgpqk", query_latent, key_latent, preferred_element_type=jnp.float32
    )
    scores = (
        scores
        + jnp.einsum("sqgpr,skr->sgpqk", query_rope, key_rope, preferred_element_type=jnp.float32)
    ) * scaling
    if diagonal:
        length = scores.shape[-1]
        causal = jnp.arange(length)[None, :] <= jnp.arange(length)[:, None]
        scores = jnp.where(causal, scores, NEG_FILL)
    return scores


def merge_block(running, key_block, query_latent, query_rope, scaling, diagonal):
    top_score, row_total, accumulated = running
    key_latent, key_rope = key_block
    scores = block_scores(query_latent, query_rope, key_latent, key_rope, scaling, diagonal)
    new_top = jnp.maximum(top_score, jnp.max(scores, -1))
    rescale = jnp.exp(top_score - new_top)
    weights = jnp.exp(scores - new_top[..., None])
    row_total = row_total * rescale + jnp.sum(weights, -1)
    accumulated = accumulated * rescale[..., None] + jnp.einsum(
        "sgpqk,skgf->sgpqf",
        weights.astype(jnp.bfloat16),
        key_latent,
        preferred_element_type=jnp.float32,
    )
    return (new_top, row_total, accumulated)


def grad_block(key_block, key_grads, query_grads, context, scaling, diagonal):
    key_latent, key_rope = key_block
    latent_grad, rope_grad = key_grads
    qlat_grad, qrope_grad = query_grads
    query_latent, query_rope, out_latent_grad, log_total, row_delta = context
    scores = block_scores(query_latent, query_rope, key_latent, key_rope, scaling, diagonal)
    probability = jnp.exp(scores - log_total[..., None])
    latent_grad = latent_grad + jnp.einsum(
        "sgpqk,sgpqf->skgf",
        probability.astype(jnp.bfloat16),
        out_latent_grad,
        preferred_element_type=jnp.float32,
    )
    prob_grad = jnp.einsum(
        "sgpqf,skgf->sgpqk", out_latent_grad, key_latent, preferred_element_type=jnp.float32
    )
    score_grad = (probability * (prob_grad - row_delta[..., None])).astype(jnp.bfloat16)
    qlat_grad = qlat_grad + scaling * jnp.einsum(
        "sgpqk,skgf->sqgpf", score_grad, key_latent, preferred_element_type=jnp.float32
    )
    qrope_grad = qrope_grad + scaling * jnp.einsum(
        "sgpqk,skr->sqgpr", score_grad, key_rope, preferred_element_type=jnp.float32
    )
    latent_grad = latent_grad + scaling * jnp.einsum(
        "sgpqk,sqgpf->skgf", score_grad, query_latent, preferred_element_type=jnp.float32
    )
    rope_grad = rope_grad + scaling * jnp.einsum(
        "sgpqk,sqgpr->skr", score_grad, query_rope, preferred_element_type=jnp.float32
    )
    return ((latent_grad, rope_grad), (qlat_grad, qrope_grad))


def pass_grads(key_grads):
    return (
        from_behind(key_grads[0].astype(jnp.bfloat16), "seq", 1).astype(jnp.float32),
        from_behind(key_grads[1].astype(jnp.bfloat16), "seq", 1).astype(jnp.float32),
    )


def local(
    tokens,
    out_grad,
    group_id,
    group_weight,
    gain_attn,
    w_query,
    w_qrope,
    w_latent,
    w_krope,
    w_ukey,
    w_uval,
    w_out,
    gain_ffn,
    w_gate,
    w_up,
    w_down,
):
    seq_count, block_len, model_width = tokens.shape
    token_rows = seq_count * block_len
    per_group = H // GROUPS
    scaling = (HD + ROPE) ** (-0.5)
    cycle_size = lax.axis_size("seq")
    cycle_index = lax.axis_index("seq")
    attn_set = (
        lax.all_gather(gain_attn.astype(jnp.bfloat16), ("seq", "batch"), axis=0, tiled=True),
        lax.all_gather(w_query.astype(jnp.bfloat16), ("seq", "batch"), axis=0, tiled=True),
        lax.all_gather(w_qrope.astype(jnp.bfloat16), ("seq", "batch"), axis=0, tiled=True),
        lax.all_gather(w_latent.astype(jnp.bfloat16), ("seq", "batch"), axis=0, tiled=True),
        lax.all_gather(w_krope.astype(jnp.bfloat16), ("seq", "batch"), axis=0, tiled=True),
        lax.all_gather(w_ukey.astype(jnp.bfloat16), ("seq", "batch"), axis=0, tiled=True),
        lax.all_gather(w_uval.astype(jnp.bfloat16), ("seq", "batch"), axis=0, tiled=True),
        lax.all_gather(w_out.astype(jnp.bfloat16), ("seq", "batch"), axis=0, tiled=True),
    )
    gain_a, query_w, qrope_w, latent_w, krope_w, ukey_w, uval_w, out_w = attn_set
    gain_a32 = gain_a.astype(jnp.float32)
    local_pos = (cycle_index * block_len + jnp.arange(block_len)).astype(jnp.float32)
    position = local_pos[None, :]
    inputs = tokens.reshape(token_rows, model_width).astype(jnp.float32)
    inverse_a, normed = norm_apply(inputs, gain_a32)
    normed = normed.astype(jnp.bfloat16)
    queries = matmul(normed, query_w).astype(jnp.bfloat16)
    query_rope = rotate(
        matmul(normed, qrope_w).reshape(seq_count, block_len, H, ROPE), position, 1.0
    ).astype(jnp.bfloat16)
    latent = matmul(normed, latent_w).astype(jnp.bfloat16)
    key_rope = rotate(
        matmul(normed, krope_w).reshape(seq_count, block_len, 1, ROPE), position, 1.0
    )[:, :, 0].astype(jnp.bfloat16)
    ukey_heads = ukey_w.reshape(H, HD, LAT)
    query_latent = jnp.einsum(
        "rhe,hef->rhf",
        queries.reshape(token_rows, H, HD),
        ukey_heads,
        preferred_element_type=jnp.float32,
    ).astype(jnp.bfloat16)
    query_latent = query_latent.reshape(seq_count, block_len, GROUPS, per_group, LAT)
    query_rope = query_rope.reshape(seq_count, block_len, GROUPS, per_group, ROPE)
    own_keys = (latent.reshape(seq_count, block_len, GROUPS, LAT), key_rope)
    state_shape = (seq_count, GROUPS, per_group, block_len)
    start_state = (
        jnp.full(state_shape, NEG_FILL, jnp.float32),
        jnp.zeros(state_shape, jnp.float32),
        jnp.zeros(state_shape + (LAT,), jnp.float32),
    )
    running = merge_block(start_state, own_keys, query_latent, query_rope, scaling, True)

    def forward_turn(carry_in, turn_index):
        key_block, running_in = carry_in
        key_block = from_behind_2((key_block[0], key_block[1]), "seq", 1)

        def merge_live(previous):
            return merge_block(previous, key_block, query_latent, query_rope, scaling, False)

        def merge_skip(previous):
            return previous

        running_out = lax.cond(turn_index <= cycle_index, merge_live, merge_skip, running_in)
        saved_keys = None
        return ((key_block, running_out), saved_keys)

    (last_keys, running), stored = lax.scan(
        forward_turn, (own_keys, running), jnp.arange(1, cycle_size)
    )
    top_score, row_total, accumulated = running
    out_latent_f = accumulated / row_total[..., None]
    log_total = top_score + jnp.log(row_total)
    out_latent = out_latent_f.astype(jnp.bfloat16)
    uval_heads = uval_w.reshape(GROUPS, per_group, HD, LAT)
    head_out = (
        jnp.einsum("sgpqf,gpef->sqgpe", out_latent, uval_heads, preferred_element_type=jnp.float32)
        .astype(jnp.bfloat16)
        .reshape(token_rows, H * HD)
    )
    residual = inputs + matmul(head_out, out_w)
    ffn_set = (
        lax.all_gather(gain_ffn.astype(jnp.bfloat16), ("seq", "batch"), axis=0, tiled=True),
        lax.all_gather(w_gate.astype(jnp.bfloat16), ("seq", "batch"), axis=0, tiled=True),
        lax.all_gather(w_up.astype(jnp.bfloat16), ("seq", "batch"), axis=0, tiled=True),
        lax.all_gather(w_down.astype(jnp.bfloat16), ("seq", "batch"), axis=0, tiled=True),
    )
    gain_f, gate_w, up_w, down_w = ffn_set
    gain_f32 = gain_f.astype(jnp.float32)
    inverse_f, normed_f = norm_apply(residual, gain_f32)
    normed_f = normed_f.astype(jnp.bfloat16)
    gate_pre = matmul(normed_f, gate_w)
    up_pre = matmul(normed_f, up_w)
    sigmoid = jax.nn.sigmoid(gate_pre)
    activated = gate_pre * sigmoid
    hidden = (activated * up_pre).astype(jnp.bfloat16)
    output = residual + matmul(hidden, down_w)
    result = output.astype(jnp.bfloat16).reshape(seq_count, block_len, model_width)
    domains = jnp.arange(group_weight.shape[0])
    seq_weight = jnp.sum(
        jnp.where(group_id[:, None] == domains[None, :], group_weight[None, :], 0.0), -1
    )
    top_grad = (out_grad.astype(jnp.float32) * seq_weight[:, None, None]).reshape(
        token_rows, model_width
    )
    down_in = top_grad.astype(jnp.bfloat16)
    hidden_grad = right_inner(down_in, down_w)
    gate_grad = (hidden_grad * up_pre * sigmoid * (1.0 + gate_pre * (1.0 - sigmoid))).astype(
        jnp.bfloat16
    )
    up_grad = (hidden_grad * activated).astype(jnp.bfloat16)
    normed_grad = right_inner(gate_grad, gate_w) + right_inner(up_grad, up_w)
    back_f, grad_gain_f = norm_grad(residual, inverse_f, gain_f32, normed_grad)
    residual_grad = top_grad + back_f
    attn_in = residual_grad.astype(jnp.bfloat16)
    head_grad = (
        right_inner(attn_in, out_w)
        .astype(jnp.bfloat16)
        .reshape(seq_count, block_len, GROUPS, per_group, HD)
    )
    grad_uval = jnp.einsum(
        "sgpqf,sqgpe->gpef", out_latent, head_grad, preferred_element_type=jnp.float32
    ).reshape(H * HD, LAT)
    out_latent_grad = jnp.einsum(
        "sqgpe,gpef->sgpqf", head_grad, uval_heads, preferred_element_type=jnp.float32
    ).astype(jnp.bfloat16)
    row_delta = jnp.sum(out_latent_grad.astype(jnp.float32) * out_latent_f, -1)
    context = (query_latent, query_rope, out_latent_grad, log_total, row_delta)
    zero_keys = (
        jnp.zeros((seq_count, block_len, GROUPS, LAT), jnp.float32),
        jnp.zeros((seq_count, block_len, ROPE), jnp.float32),
    )
    zero_query = (
        jnp.zeros(query_latent.shape, jnp.float32),
        jnp.zeros(query_rope.shape, jnp.float32),
    )
    key_grads, query_grads = grad_block(own_keys, zero_keys, zero_query, context, scaling, True)

    def backward_turn(carry_in, payload):
        key_block, key_part, query_part = carry_in
        turn_index, saved_keys = payload
        key_block = from_behind_2((key_block[0], key_block[1]), "seq", 1)
        key_part = pass_grads(key_part)

        def grads_live(previous):
            return grad_block(key_block, previous[0], previous[1], context, scaling, False)

        def grads_skip(previous):
            return previous

        key_part, query_part = lax.cond(
            turn_index <= cycle_index, grads_live, grads_skip, (key_part, query_part)
        )
        return ((key_block, key_part, query_part), None)

    (final_keys, key_grads, query_grads), unused = lax.scan(
        backward_turn, (own_keys, key_grads, query_grads), (jnp.arange(1, cycle_size), stored)
    )
    key_grads = pass_grads(key_grads)
    latent_grad = key_grads[0].astype(jnp.bfloat16).reshape(token_rows, GROUPS * LAT)
    krope_grad = (
        rotate(key_grads[1][:, :, None, :], position, -1.0)[:, :, 0]
        .astype(jnp.bfloat16)
        .reshape(token_rows, ROPE)
    )
    qlat_grad = query_grads[0].astype(jnp.bfloat16).reshape(token_rows, H, LAT)
    qrope_grad = (
        rotate(query_grads[1].reshape(seq_count, block_len, H, ROPE), position, -1.0)
        .astype(jnp.bfloat16)
        .reshape(token_rows, H * ROPE)
    )
    grad_ukey = jnp.einsum(
        "rhe,rhf->hef",
        queries.reshape(token_rows, H, HD),
        qlat_grad,
        preferred_element_type=jnp.float32,
    ).reshape(H * HD, LAT)
    query_grad = (
        jnp.einsum("rhf,hef->rhe", qlat_grad, ukey_heads, preferred_element_type=jnp.float32)
        .astype(jnp.bfloat16)
        .reshape(token_rows, H * HD)
    )
    normed_grad_a = (
        right_inner(query_grad, query_w)
        + right_inner(qrope_grad, qrope_w)
        + right_inner(latent_grad, latent_w)
        + right_inner(krope_grad, krope_w)
    )
    back_a, grad_gain_a = norm_grad(inputs, inverse_a, gain_a32, normed_grad_a)
    input_grad = (residual_grad + back_a).reshape(seq_count, block_len, model_width)
    gain_part = (
        lax.psum_scatter(grad_gain_a, ("seq", "batch"), scatter_dimension=0, tiled=True),
        lax.psum_scatter(grad_gain_f, ("seq", "batch"), scatter_dimension=0, tiled=True),
    )
    model_part = lax.psum_scatter(
        jnp.concatenate(
            [
                left_inner(normed, query_grad),
                left_inner(normed, qrope_grad),
                left_inner(normed, latent_grad),
                left_inner(normed, krope_grad),
                left_inner(normed_f, gate_grad),
                left_inner(normed_f, up_grad),
            ],
            1,
        ),
        ("seq", "batch"),
        scatter_dimension=0,
        tiled=True,
    )
    head_part = lax.psum_scatter(
        jnp.concatenate([grad_ukey, grad_uval, left_inner(head_out, attn_in)], 1),
        ("seq", "batch"),
        scatter_dimension=0,
        tiled=True,
    )
    down_part = lax.psum_scatter(
        left_inner(hidden, down_in), ("seq", "batch"), scatter_dimension=0, tiled=True
    )
    edge_one = H * HD
    edge_two = edge_one + H * ROPE
    edge_three = edge_two + GROUPS * LAT
    edge_four = edge_three + ROPE
    edge_five = edge_four + FF
    part_query = model_part[:, :edge_one]
    part_qrope = model_part[:, edge_one:edge_two]
    part_latent = model_part[:, edge_two:edge_three]
    part_krope = model_part[:, edge_three:edge_four]
    part_gate = model_part[:, edge_four:edge_five]
    part_up = model_part[:, edge_five:]
    part_ukey = head_part[:, :LAT]
    part_uval = head_part[:, LAT : 2 * LAT]
    part_out = head_part[:, 2 * LAT :]
    return (
        result,
        input_grad,
        gain_part[0],
        part_query,
        part_qrope,
        part_latent,
        part_krope,
        part_ukey,
        part_uval,
        part_out,
        gain_part[1],
        part_gate,
        part_up,
        down_part,
    )


def solution(mesh):
    return jax.shard_map(
        local,
        mesh=mesh,
        in_specs=(
            P("batch", "seq", None),
            P("batch", "seq", None),
            P("batch"),
            P(),
            P(("seq", "batch")),
            P(("seq", "batch"), None),
            P(("seq", "batch"), None),
            P(("seq", "batch"), None),
            P(("seq", "batch"), None),
            P(("seq", "batch"), None),
            P(("seq", "batch"), None),
            P(("seq", "batch"), None),
            P(("seq", "batch")),
            P(("seq", "batch"), None),
            P(("seq", "batch"), None),
            P(("seq", "batch"), None),
        ),
        out_specs=(
            P("batch", "seq", None),
            P("batch", "seq", None),
            P(("seq", "batch")),
            P(("seq", "batch"), None),
            P(("seq", "batch"), None),
            P(("seq", "batch"), None),
            P(("seq", "batch"), None),
            P(("seq", "batch"), None),
            P(("seq", "batch"), None),
            P(("seq", "batch"), None),
            P(("seq", "batch")),
            P(("seq", "batch"), None),
            P(("seq", "batch"), None),
            P(("seq", "batch"), None),
        ),
        check_vma=False,
    )
```

profile of v0, /device:TPU:0, one launch (start us, length us, event | category | flops | bytes accessed | tf_op | source)
XLA Modules:
  0.0 1741.1 jit_solution(17809240214518602237)
XLA Ops:
  19.2 42.0 %all-reduce.5 = (bf16[1024]{0:T(1024)(128)(2,1)S(1)}, bf16[1024]{0:T(1024)(128)(2,1)S(1)}) all-reduce(bf16[1024]{0:T(1024)(128)(2,1)S(1)} %dynamic-update-slice, bf16[1024]{0:T(1024)(128)(2,1)S(1)} %dynamic-update-slice.1), channel_id=1, replica_groups=mesh['seq'=8,'batch'=4] {'seq','batch'}, use_global_device_ids=true, to_apply=%add | all-reduce | flops 2048 | bytes 8192
  61.9 68.4 %all_gather.38 = bf16[1024,64]{1,0:T(8,128)(2,1)S(1)} all-gather(bf16[32,64]{1,0:T(8,128)(2,1)S(1)} %convert_element_type.282), channel_id=1, replica_groups=mesh['seq'=8,'batch'=4] {'seq','batch'}, dimensions={0}, use_global_device_ids=true | all-gather | bytes 135168 | tf_op jit(solution)/shard_map/all_gather | solution.py:178
  134.7 73.5 %all_gather.42 = bf16[1024,256]{1,0:T(8,128)(2,1)} all-gather(bf16[32,256]{1,0:T(8,128)(2,1)S(1)} %convert_element_type.298), channel_id=1, replica_groups=mesh['seq'=8,'batch'=4] {'seq','batch'}, dimensions={0}, use_global_device_ids=true | all-gather | bytes 540672 | tf_op jit(solution)/shard_map/all_gather | solution.py:180
  208.2 71.4 %all_gather.40 = bf16[1024,256]{1,0:T(8,128)(2,1)S(1)} all-gather(bf16[32,256]{1,0:T(8,128)(2,1)S(1)} %convert_element_type.289), channel_id=1, replica_groups=mesh['seq'=8,'batch'=4] {'seq','batch'}, dimensions={0}, use_global_device_ids=true | all-gather | bytes 540672 | tf_op jit(solution)/shard_map/all_gather | solution.py:179
  284.6 2.9 copy.108
  292.2 81.0 %while.38 = (s32[]{:T(128)}, bf16[1,128,2,256]{3,1,2,0:T(8,128)(2,1)}, bf16[1,128,64]{1,2,0:T(8,128)(2,1)}, f32[1,2,8,128]{3,2,1,0:T(8,128)}, f32[1,2,8,128]{3,2...) while((s32[]{:T(128)}, ...), condition=%wide.region_8.9_spmd, body=%wide.region_3.8_spmd.sunk | while | flops 304879616 | bytes 12140963 | solution.py:230
  298.0 4.6 collective-permute-start
  302.6 7.9 collective-permute-start.1
  313.7 3.6 collective-permute-start
  317.3 8.5 collective-permute-start.1
  331.0 4.2 collective-permute-start.1
  338.4 5.2 collective-permute-start
  343.5 4.3 collective-permute-start.1
  351.1 3.0 collective-permute-start
  354.1 6.4 collective-permute-start.1
  365.6 4.2 collective-permute-start.1
  379.6 4.7 fusion.153
  384.3 3.9 all-gather.16.cloned.1.call-done
  388.2 4.7 fusion.152
  392.9 64.2 %all-gather.20.cloned.1.call-done = bf16[2816,1024]{1,0:T(8,128)(2,1)} async-done(((bf16[88,1024]{1,0:T(8,128)(2,1)}), bf16[2816,1024]{1,0:T(8,128)(2,1)}) %all-gather.20.cloned.1.call-update) | async-done | bytes 5767184 | tf_op jit(solution)/shard_map/all_gather | solution.py:248
  457.1 7.5 multiply_convert_fusion
  466.6 5.5 multiply_reduce_fusion.1
  474.6 3.5 multiply_reduce_fusion
  493.3 2.9 copy.125
  497.5 119.6 %while.39 = (s32[]{:T(128)}, bf16[1,128,2,256]{3,1,2,0:T(8,128)(2,1)}, bf16[1,128,64]{1,2,0:T(8,128)(2,1)}, f32[1,128,2,256]{3,1,2,0:T(8,128)S(1)}, f32[1,128,64...) while((s32[]{:T(128)}, ...), condition=%wide.region_16.17_spmd, body=%wide.region_13.16_spmd.sunk | while | flops 775258112 | bytes 38781536 | solution.py:318
  498.6 3.0 collective-permute-start.2
  502.7 3.4 collective-permute-start.3
  511.5 7.0 collective-permute-start.4
  522.0 3.4 collective-permute-start.3
  530.9 9.6 collective-permute-start.2
  541.3 3.6 collective-permute-start.3
  550.4 3.0 collective-permute-start.2
  554.2 6.8 collective-permute-start.5
  561.0 3.6 collective-permute-start.3
  573.5 10.3 collective-permute-start.3
  601.0 4.2 collective-permute-start.4
  608.7 3.6 collective-permute-start.3
  622.7 6.2 pad_maximum_fusion
  628.9 6.6 copy.178
  637.0 5.9 collective-permute-start.6
  646.3 5.9 fusion.157
  652.2 5.9 fusion.156
  662.6 41.2 %concatenate.85 = f32[1024,8256]{1,0:T(8,128)} concatenate(f32[1024,1024]{1,0:T(8,128)} %fusion.95, f32[1024,1024]{1,0:T(8,128)} %fusion.93, f32[1024,512]{1,0:T(8,128)S(1)} %fusion.91, f32[1024,64]{1,0:T(8,128)S(1)} %fusion.97, f32[1024,2816]{1,0:T(8,128)} %fusion.156, f32[1024,2816]{1,0:T(8,128)} %fusion.157), dimensions={1} | concatenate | bytes 67633152 | tf_op jit(solution)/shard_map/concatenate | solution.py:358
  705.0 6.5 fusion.99
  715.8 4.4 fusion.54
  721.2 42.9 %all-reduce.4 = (f32[1024]{0:T(1024)S(1)}, f32[1024]{0:T(1024)S(1)}) all-reduce(f32[1024]{0:T(1024)S(1)} %get-tuple-element.341, f32[1024]{0:T(1024)S(1)} %copy-done.76), channel_id=2, replica_groups=mesh['seq'=8,'batch'=4] {'seq','batch'}, use_global_device_ids=true, to_apply=%region_19.20.clone | all-reduce | flops 2048 | bytes 16384
  769.3 711.4 %reduce-scatter.6.cloned.1.call-done = f32[32,8256]{1,0:T(8,128)} async-done(((f32[1024,8256]{1,0:T(8,128)}), f32[32,8256]{1,0:T(8,128)}) %reduce-scatter.6.cloned.1.call-update) | async-done | bytes 1056784 | tf_op jit(solution)/shard_map/reduce_scatter | solution.py:357
  1487.4 246.4 %reduce-scatter.8.cloned.1.call-done = f32[88,1024]{1,0:T(8,128)} async-done(((f32[2816,1024]{1,0:T(8,128)}), f32[88,1024]{1,0:T(8,128)}) %reduce-scatter.8.cloned.1.call-update) | async-done | bytes 360464 | tf_op jit(solution)/shard_map/reduce_scatter | solution.py:379
  (431 shorter events, 162.7 us)
Async XLA Ops:
  7.3 272.3 %all-gather.8.cloned.1.call-start = ((), (), s32[]{:S(2)}) async-start(), calls=%async_computation.3 | async-start | bytes 1081344 | tf_op jit(solution)/shard_map/all_gather | solution.py:177
  8.9 273.4 %all-gather.10.cloned.1.call-start = ((), (), s32[]{:S(2)}) async-start(), calls=%async_computation.4 | async-start | bytes 2162688 | tf_op jit(solution)/shard_map/all_gather | solution.py:175
  10.5 274.1 %all-gather.12.cloned.1.call-start = ((), (), s32[]{:S(2)}) async-start(), calls=%async_computation.5 | async-start | bytes 2162688 | tf_op jit(solution)/shard_map/all_gather | solution.py:176
  12.1 363.8 %all-gather.14.cloned.1.call-start = ((), (), s32[]{:S(2)}) async-start(), calls=%async_computation.6 | async-start | bytes 2162688 | tf_op jit(solution)/shard_map/all_gather | solution.py:181
  13.8 365.8 %all-gather.18.cloned.1.call-start = ((), (), s32[]{:S(2)}) async-start(), calls=%async_computation.8 | async-start | bytes 5947392 | tf_op jit(solution)/shard_map/all_gather | solution.py:247
  15.5 372.7 %all-gather.16.cloned.1.call-start = ((), (), s32[]{:S(2)}) async-start(), calls=%async_computation.7 | async-start | bytes 5947392 | tf_op jit(solution)/shard_map/all_gather | solution.py:246
  17.2 439.8 %all-gather.20.cloned.1.call-start = ((), (), s32[]{:S(2)}) async-start(), calls=%async_computation.9 | async-start | bytes 5947392 | tf_op jit(solution)/shard_map/all_gather | solution.py:248
  18.0 748.3 %reduce-scatter.10.cloned.1.call-start = ((), (), s32[]{:S(2)}) async-start(), calls=%async_computation.12 | async-start | bytes 6488064
  298.0 15.0 collective-permute-start
  302.6 9.8 collective-permute-start.1
  313.7 14.7 collective-permute-start
  317.3 10.4 collective-permute-start.1
  329.0 8.7 collective-permute-start
  331.0 6.1 collective-permute-start.1
  338.4 12.0 collective-permute-start
  343.5 6.3 collective-permute-start.1
  351.1 11.9 collective-permute-start
  354.1 8.3 collective-permute-start.1
  363.7 8.7 collective-permute-start
  365.6 6.2 collective-permute-start.1
  498.4 10.9 collective-permute-start.4
  498.6 11.6 collective-permute-start.2
  502.4 5.6 collective-permute-start.5
  502.7 6.0 collective-permute-start.3
  511.5 17.1 collective-permute-start.4
  518.5 11.0 collective-permute-start.2
  522.0 6.0 collective-permute-start.3
  530.9 17.2 collective-permute-start.4
  530.9 18.1 %collective-permute-start.2 = (bf16[1,128,2,256]{3,1,2,0:T(8,128)(2,1)}, bf16[1,128,2,256]{3,1,2,0:T(8,128)(2,1)S(1)}, u32[]{:S(2)}, u32[]{:S(2)}) collective-permute-start(bf16[1,128,2,256]{3,1,2,0:T(8,128)(2,1)} %get-tuple-element.657), channel_id=1, source_target_pairs={{0,4},{4,8},{8,12},{12,16},{16,20},{20,24},{24,28},{1,5},{5,9},{9,... | collective-permute-start | bytes 393224 | tf_op jit(solution)/shard_map/while/body/eval_jaxpr/ppermute | solution.py:27
  541.3 6.1 collective-permute-start.3
  550.4 17.3 collective-permute-start.4
  550.4 18.2 %collective-permute-start.2 = (bf16[1,128,2,256]{3,1,2,0:T(8,128)(2,1)}, bf16[1,128,2,256]{3,1,2,0:T(8,128)(2,1)S(1)}, u32[]{:S(2)}, u32[]{:S(2)}) collective-permute-start(bf16[1,128,2,256]{3,1,2,0:T(8,128)(2,1)} %get-tuple-element.657), channel_id=1, source_target_pairs={{0,4},{4,8},{8,12},{12,16},{16,20},{20,24},{24,28},{1,5},{5,9},{9,... | collective-permute-start | bytes 393224 | tf_op jit(solution)/shard_map/while/body/eval_jaxpr/ppermute | solution.py:27
  554.2 12.3 collective-permute-start.5
  561.0 6.1 collective-permute-start.3
  570.0 17.0 collective-permute-start.4
  570.0 17.9 %collective-permute-start.2 = (bf16[1,128,2,256]{3,1,2,0:T(8,128)(2,1)}, bf16[1,128,2,256]{3,1,2,0:T(8,128)(2,1)S(1)}, u32[]{:S(2)}, u32[]{:S(2)}) collective-permute-start(bf16[1,128,2,256]{3,1,2,0:T(8,128)(2,1)} %get-tuple-element.657), channel_id=1, source_target_pairs={{0,4},{4,8},{8,12},{12,16},{16,20},{20,24},{24,28},{1,5},{5,9},{9,... | collective-permute-start | bytes 393224 | tf_op jit(solution)/shard_map/while/body/eval_jaxpr/ppermute | solution.py:27
  573.5 12.3 collective-permute-start.5
  573.5 12.9 collective-permute-start.3
  589.3 9.5 collective-permute-start.4
  589.3 10.4 collective-permute-start.2
  601.0 14.4 collective-permute-start.4
  605.2 11.2 collective-permute-start.2
  608.7 5.5 collective-permute-start.5
  608.7 6.2 collective-permute-start.3
  635.5 845.2 %reduce-scatter.6.cloned.1.call-start = ((), (), s32[]{:S(2)}) async-start(), calls=%async_computation.10 | async-start | bytes 35143680 | tf_op jit(solution)/shard_map/reduce_scatter | solution.py:357
  636.2 24.7 %collective-permute-start.7 = (bf16[1,128,64]{1,2,0:T(8,128)(2,1)S(1)}, bf16[1,128,64]{1,2,0:T(8,128)(2,1)S(1)}, u32[]{:S(2)}, u32[]{:S(2)}) collective-permute-start(bf16[1,128,64]{1,2,0:T(8,128)(2,1)S(1)} %convert_element_type.331), channel_id=1, source_target_pairs={{0,4},{4,8},{8,12},{12,16},{16,20},{20,24},{24,28},{28,0},{1,5},{5... | collective-permute-start | bytes 49160 | tf_op jit(solution)/shard_map/ppermute | solution.py:21
  637.0 24.4 %collective-permute-start.6 = (bf16[1,128,2,256]{1,3,2,0:T(8,128)(2,1)}, bf16[1,128,2,256]{1,3,2,0:T(8,128)(2,1)S(1)}, u32[]{:S(2)}, u32[]{:S(2)}) collective-permute-start(bf16[1,128,2,256]{1,3,2,0:T(8,128)(2,1)} %copy.126), channel_id=1, source_target_pairs={{0,4},{4,8},{8,12},{12,16},{16,20},{20,24},{24,28},{28,0},{1,5},{5... | collective-permute-start | bytes 393224 | tf_op jit(solution)/shard_map/ppermute | solution.py:21
  703.8 1030.0 %reduce-scatter.8.cloned.1.call-start = ((), (), s32[]{:S(2)}) async-start(), calls=%async_computation.11 | async-start | bytes 11894784 | tf_op jit(solution)/shard_map/reduce_scatter | solution.py:379
  (86 other events, 1960.3 us)
Sparse Core Ops, SparseCore 0:
  11.6 56.6 all-gather.7
  71.8 55.8 all-gather.9
  131.2 55.3 all-gather.11
  190.0 55.8 all-gather.13
  248.6 68.7 all-gather.17
  320.6 67.4 all-gather.15
  391.0 66.0 all-gather.19
  635.6 121.0 reduce-scatter.9
  759.1 721.6 reduce-scatter.5
  1483.5 250.3 reduce-scatter.7
where the time goes:
time: 1750 us; the launch traced here: 1740 us
  waiting for transfers between devices  1030 us (59%)
  blocking collectives  298 us (17%)
  starting transfers between devices  141 us (8%)
  local copies, waits for them, and re-layouts  115 us (7%)
  matrix products  86.8 us (5%)
  other arithmetic  47.9 us (3%)
    reduce_scatter x1, waiting for transfers between devices, local(): lax.psum_scatter(jnp.concatenate([left_inner(normed, query_grad), left_in...  711 us
    reduce_scatter x1, waiting for transfers between devices, local(): lax.psum_scatter(left_inner(hidden, down_in), ('seq', 'batch'), scatter_d...  246 us
    ppermute x28, starting transfers between devices, from_behind_2(): return lax.ppermute(x, axis, pairs)  116 us
    unnamed x2, blocking collectives  84.9 us
    all_gather x1, blocking collectives, local(): lax.all_gather(w_uval.astype(jnp.bfloat16), ('seq', 'batch'), axis=0, til...  73.5 us
    all_gather x1, blocking collectives, local(): lax.all_gather(w_ukey.astype(jnp.bfloat16), ('seq', 'batch'), axis=0, til...  71.4 us
    all_gather x1, blocking collectives, local(): lax.all_gather(w_krope.astype(jnp.bfloat16), ('seq', 'batch'), axis=0, ti...  68.4 us
    all_gather x1, waiting for transfers between devices, local(): lax.all_gather(w_down.astype(jnp.bfloat16), ('seq', 'batch'), axis=0, til...  64.2 us
  transfers between devices with their start and end apart: 54, of which 4 were waited for; matrix products, arithmetic and copies ran while one was open for 10% of the time, Pallas kernels for 0%

commit v1 on v0

v1 whole, which is shorter than its diff:
```python
import jax
import jax.numpy as jnp
from jax import lax
from jax.sharding import PartitionSpec as P

FF = 2816
H = 16
HD = 64
GROUPS = 2
LAT = 256
ROPE = 64
PER_GROUP = H // GROUPS

EPSILON = 1e-05
ROTARY_BASE = 10000.0
NEG_FILL = -1e30
BF = jnp.bfloat16
F32 = jnp.float32


def mm(a, b):
    return jnp.dot(a, b, preferred_element_type=F32)


def mm_tn(a, b):
    return lax.dot_general(a, b, (((0,), (0,)), ((), ())), preferred_element_type=F32)


def mm_nt(a, b):
    return lax.dot_general(a, b, (((1,), (1,)), ((), ())), preferred_element_type=F32)


def rms(v, g):
    inv = lax.rsqrt(jnp.mean(v * v, -1, keepdims=True) + EPSILON)
    return inv, v * inv * g


def rms_grad(v, inv, g, dn):
    scaled = dn * g
    back = inv * scaled - v * (inv * inv * inv) * jnp.mean(scaled * v, -1, keepdims=True)
    return back, jnp.sum(dn * v * inv, 0)


def rotate(v, cosine, sine):
    half = v.shape[-1] // 2
    lo, hi = v[..., :half], v[..., half:]
    return jnp.concatenate([lo * cosine - hi * sine, lo * sine + hi * cosine], -1)


def seq_gather(v):
    return lax.all_gather(v, "seq", axis=0, tiled=True)


def seq_sum(v):
    return lax.psum_scatter(v.astype(BF), "seq", scatter_dimension=0, tiled=True).astype(F32)


def batch_gather(v):
    return lax.all_gather(v, "batch", axis=0, tiled=True)


def batch_sum(v):
    return lax.psum_scatter(v.astype(BF), "batch", scatter_dimension=0, tiled=True).astype(F32)


def local(
    tokens,
    out_grad,
    group_id,
    group_weight,
    gain_attn,
    w_query,
    w_qrope,
    w_latent,
    w_krope,
    w_ukey,
    w_uval,
    w_out,
    gain_ffn,
    w_gate,
    w_up,
    w_down,
):
    ns, nb = lax.axis_size("seq"), lax.axis_size("batch")
    seq_count, rows, width = tokens.shape
    shard = w_query.shape[0]
    length = rows * ns
    hl = H // ns
    fl = FF // ns
    qw, rw = hl * HD, hl * ROPE
    scaling = (HD + ROPE) ** (-0.5)

    def columns(w, blocks):
        return w.astype(BF).reshape(shard, blocks, -1).transpose(1, 0, 2)

    lat_cols = jnp.repeat(columns(w_latent, GROUPS), ns // GROUPS, axis=0)
    kr_cols = jnp.broadcast_to(w_krope.astype(BF)[None], (ns, shard, ROPE))
    send = jnp.concatenate(
        [columns(w_query, ns), columns(w_qrope, ns), lat_cols, kr_cols, columns(w_gate, ns), columns(w_up, ns)], -1
    )
    got = lax.all_to_all(send, "seq", 0, 0)
    wide = send.shape[-1]
    full = lax.all_gather(got, "batch", axis=1).reshape(width, wide)
    attn_w = qw + rw + LAT + ROPE
    wcat, wgu = full[:, :attn_w], full[:, attn_w:]
    ukey = batch_gather(w_ukey.astype(BF))
    uval = batch_gather(w_uval.astype(BF))
    wout = batch_gather(w_out.astype(BF))
    wdown = batch_gather(w_down.astype(BF))
    gains = lax.all_gather(
        jnp.stack([gain_attn, gain_ffn]).astype(BF), ("seq", "batch"), axis=1, tiled=True
    ).astype(F32)
    gain_a, gain_f = gains[0], gains[1]

    x = tokens.reshape(rows, width)
    domains = jnp.arange(group_weight.shape[0])
    seq_weight = jnp.sum(jnp.where(group_id[:, None] == domains[None, :], group_weight[None, :], 0.0), -1)
    gy = (out_grad.astype(F32) * seq_weight[:, None, None]).reshape(rows, width)
    dy_all = seq_gather(gy.astype(BF))
    x_all = seq_gather(x)
    x32 = x.astype(F32)

    position = jnp.arange(length).astype(F32)
    freq = ROTARY_BASE ** (-jnp.arange(ROPE // 2).astype(F32) * 2.0 / ROPE)
    angles = position[:, None] * freq
    cosine, sine = jnp.cos(angles), jnp.sin(angles)

    _, normed = rms(x_all.astype(F32), gain_a)
    a_all = normed.astype(BF)
    qkv = mm(a_all, wcat)
    q = qkv[:, :qw].astype(BF)
    qr = rotate(qkv[:, qw : qw + rw].reshape(length, hl, ROPE), cosine[:, None], sine[:, None]).astype(BF)
    c = qkv[:, qw + rw : qw + rw + LAT].astype(BF)
    kr = rotate(qkv[:, qw + rw + LAT :], cosine, sine).astype(BF)
    causal = jnp.arange(length)[None, :] <= jnp.arange(length)[:, None]

    keep = []
    outs = []
    for h in range(hl):
        uh = ukey[h * HD : (h + 1) * HD]
        vh = uval[h * HD : (h + 1) * HD]
        ql = mm(q[:, h * HD : (h + 1) * HD], uh).astype(BF)
        sc = (mm_nt(ql, c) + mm_nt(qr[:, h], kr)) * scaling
        sc = jnp.where(causal, sc, NEG_FILL)
        top = jnp.max(sc, -1, keepdims=True)
        e = jnp.exp(sc - top)
        total = jnp.sum(e, -1, keepdims=True)
        ol = mm(e.astype(BF), c) / total
        olb = ol.astype(BF)
        outs.append(mm_nt(olb, vh).astype(BF))
        keep.append((ql, ol, olb, top + jnp.log(total)))
    o = jnp.concatenate(outs, -1)
    hres = x32 + seq_sum(mm(o, wout))
    inv_f, normed_f = rms(hres, gain_f)
    b_all = seq_gather(normed_f.astype(BF))
    gu = mm(b_all, wgu)
    gate, up = gu[:, :fl], gu[:, fl:]
    sig = jax.nn.sigmoid(gate)
    act = gate * sig
    hid = (act * up).astype(BF)
    y = seq_sum(mm(hid, wdown))
    result = (hres + y).astype(BF).reshape(seq_count, rows, width)

    dhid = mm_nt(dy_all, wdown)
    dgate = (dhid * up * sig * (1.0 + gate * (1.0 - sig))).astype(BF)
    dup = (dhid * act).astype(BF)
    dgu = jnp.concatenate([dgate, dup], -1)
    db = seq_sum(mm_nt(dgu, wgu))
    g_down = batch_sum(mm_tn(hid, dy_all))
    g_gu = mm_tn(b_all, dgu)
    back_f, gg_f = rms_grad(hres, inv_f, gain_f, db)
    dres = gy + back_f
    dat_all = seq_gather(dres.astype(BF))
    g_out = mm_tn(o, dat_all)
    do = mm_nt(dat_all, wout).astype(BF)

    dqs, dqps, g_uk, g_uv = [], [], [], []
    dc = jnp.zeros((length, LAT), F32)
    dkr = jnp.zeros((length, ROPE), F32)
    for h in range(hl):
        ql, ol, olb, lse = keep[h]
        uh = ukey[h * HD : (h + 1) * HD]
        vh = uval[h * HD : (h + 1) * HD]
        doh = do[:, h * HD : (h + 1) * HD]
        g_uv.append(mm_tn(doh, olb))
        dol = mm(doh, vh).astype(BF)
        delta = jnp.sum(dol.astype(F32) * ol, -1, keepdims=True)
        sc = (mm_nt(ql, c) + mm_nt(qr[:, h], kr)) * scaling
        p = jnp.exp(jnp.where(causal, sc, NEG_FILL) - lse)
        ds = (p * (mm_nt(dol, c) - delta)).astype(BF)
        dql = (scaling * mm(ds, c)).astype(BF)
        dqps.append(rotate(scaling * mm(ds, kr), cosine, -sine).astype(BF))
        dkr = dkr + scaling * mm_tn(ds, qr[:, h])
        dc = dc + mm_tn(p.astype(BF), dol) + scaling * mm_tn(ds, ql)
        g_uk.append(mm_tn(q[:, h * HD : (h + 1) * HD], dql))
        dqs.append(mm_nt(dql, uh).astype(BF))
    dkp = rotate(dkr, cosine, -sine).astype(BF)
    gcat = jnp.concatenate(dqs + dqps + [dc.astype(BF), dkp], -1)
    da = seq_sum(mm_nt(gcat, wcat))
    g_cat = mm_tn(a_all, gcat)
    inv_a, _ = rms(x32, gain_a)
    back_a, gg_a = rms_grad(x32, inv_a, gain_a, da)
    input_grad = (dres + back_a).reshape(seq_count, rows, width)

    def wide_sum(g):
        cols = g.shape[-1]
        part = lax.psum_scatter(
            g.astype(BF).reshape(ns, nb, shard, cols), "batch", scatter_dimension=1, tiled=True
        ).reshape(ns, shard, cols)
        return lax.all_to_all(part, "seq", 0, 0)

    def spread(v):
        return v.transpose(1, 0, 2).reshape(shard, -1)

    r_gu = wide_sum(g_gu)
    r_cat = wide_sum(g_cat).astype(F32)
    p_query = spread(r_cat[:, :, :qw])
    p_qrope = spread(r_cat[:, :, qw : qw + rw])
    p_latent = spread(
        r_cat[:, :, qw + rw : qw + rw + LAT].reshape(GROUPS, ns // GROUPS, shard, LAT).sum(1)
    )
    p_krope = r_cat[:, :, qw + rw + LAT :].sum(0)
    p_gate = spread(r_gu[:, :, :fl]).astype(F32)
    p_up = spread(r_gu[:, :, fl:]).astype(F32)
    g_head = batch_sum(jnp.concatenate([jnp.concatenate(g_uk, 0), jnp.concatenate(g_uv, 0), g_out], -1))
    gg = lax.psum_scatter(jnp.stack([gg_a, gg_f]), ("seq", "batch"), scatter_dimension=1, tiled=True)
    return (
        result,
        input_grad,
        gg[0],
        p_query,
        p_qrope,
        p_latent,
        p_krope,
        g_head[:, :LAT],
        g_head[:, LAT : 2 * LAT],
        g_head[:, 2 * LAT :],
        gg[1],
        p_gate,
        p_up,
        g_down,
    )


def solution(mesh):
    token, row, flat = P("batch", "seq", None), P(("seq", "batch"), None), P(("seq", "batch"))
    return jax.shard_map(
        local,
        mesh=mesh,
        in_specs=(token, token, P("batch"), P(), flat, row, row, row, row, row, row, row, flat, row, row, row),
        out_specs=(token, token, flat, row, row, row, row, row, row, row, flat, row, row, row),
        check_vma=False,
    )
```

time: 1750 us -> 755 us (0.43)
  waiting for transfers between devices: 1030 us -> 428 us
  blocking collectives: 298 us -> 147 us
  starting transfers between devices: 141 us -> 8.11 us
  local copies, waits for them, and re-layouts: 115 us -> 50.5 us
    reduce_scatter x2 -> x6, waiting for transfers between devices: 958 us -> 138 us  [the longest x4 138 us: seq_sum(): lax.psum_scatter(v.astype(BF), 'seq', scatter_dimension=0, tiled=True)]
    unnamed x11 -> x15, waiting for transfers between devices: 0.16 us -> 237 us
    ppermute x44 -> x0, starting transfers between devices: 140 us -> none  [the longest x28 116 us: from_behind_2(): return lax.ppermute(x, axis, pairs)]
    all_gather x3 -> x5, blocking collectives: 213 us -> 128 us  [the longest x1 68.3 us: local(): lax.all_gather(jnp.stack([gain_attn, gain_ffn]).astype(BF), ('seq', 'batc...]
    unnamed x2 -> x0, blocking collectives: 84.9 us -> none
    concatenate x1 -> x3, local copies, waits for them, and re-layouts: 41.2 us -> 4.75 us  [the longest x1 4.19 us: local(): gcat = jnp.concatenate(dqs + dqps + [dc.astype(BF), dkp], -1)]
    all_gather x7 -> x5, waiting for transfers between devices: 68.1 us -> 44.2 us  [the longest x4 44.1 us: seq_gather(): return lax.all_gather(v, 'seq', axis=0, tiled=True)]
    convert_element_type x48 -> x16, other arithmetic: 33.6 us -> 11.1 us  [the longest x1 2.59 us: local(): dat_all = seq_gather(dres.astype(BF))]
  transfers between devices with their start and end apart: 54 -> 15, of which waited for: 4 -> 11; matrix products, arithmetic and copies ran while one was open for 10% -> 14% of each run, Pallas kernels for 0% -> 0%
where the time goes in v1:
time: 755 us; the launch traced here: 750 us
  waiting for transfers between devices  428 us (57%)
  blocking collectives  147 us (19%)
  matrix products  69.9 us (9%)
  local copies, waits for them, and re-layouts  50.5 us (7%)
  other arithmetic  31 us (4%)
  between operations  15.8 us (2%)
  starting transfers between devices  8.11 us (1%)
    unnamed x15, waiting for transfers between devices  237 us
    reduce_scatter x4, waiting for transfers between devices, seq_sum(): lax.psum_scatter(v.astype(BF), 'seq', scatter_dimension=0, tiled=True)  138 us
    all_gather x1, blocking collectives, local(): lax.all_gather(jnp.stack([gain_attn, gain_ffn]).astype(BF), ('seq', 'batc...  68.3 us
    all_gather x4, blocking collectives, batch_gather(): return lax.all_gather(v, 'batch', axis=0, tiled=True)  59.9 us
    all_gather x4, waiting for transfers between devices, seq_gather(): return lax.all_gather(v, 'seq', axis=0, tiled=True)  44.1 us
    dot_general x14, matrix products, mm_tn(): lax.dot_general(a, b, (((0,), (0,)), ((), ())), preferred_element_type=F32)  26.7 us
    dot_general x14, matrix products, mm_nt(): lax.dot_general(a, b, (((1,), (1,)), ((), ())), preferred_element_type=F32)  24.1 us
    dot_general x14, matrix products, mm(): return jnp.dot(a, b, preferred_element_type=F32)  19.1 us
  transfers between devices with their start and end apart: 15, of which 11 were waited for; matrix products, arithmetic and copies ran while one was open for 14% of the time, Pallas kernels for 0%

profile of v1, /device:TPU:0, one launch (start us, length us, event | category | flops | bytes accessed | tf_op | source)
XLA Modules:
  0.0 750.4 jit_solution(7348768484300673113)
XLA Ops:
  13.9 18.9 %all_to_all.15 = bf16[8,32,1280]{2,1,0:T(8,128)(2,1)S(1)} all-to-all(bf16[8,32,1280]{2,1,0:T(8,128)(2,1)S(1)} %copy.138), channel_id=1, replica_groups=mesh['seq'=8,'batch'=4] {'seq'}, dimensions={0} | all-to-all | bytes 1310720 | tf_op jit(solution)/shard_map/all_to_all | solution.py:101
  34.2 68.3 %all-gather.2 = bf16[32,32,2]{1,2,0:T(2,128)(2,1)S(1)} all-gather(bf16[1,32,2]{1,2,0:T(2,128)(2,1)S(1)} %maximum_bitcast_fusion), channel_id=1, replica_groups=mesh['seq'=8,'batch'=4] {'seq','batch'}, dimensions={0}, use_global_device_ids=true | all-gather | bytes 4224 | tf_op jit(solution)/shard_map/all_gather | solution.py:110
  102.7 13.2 %all_gather.38 = bf16[128,256]{1,0:T(8,128)(2,1)S(1)} all-gather(bf16[32,256]{1,0:T(8,128)(2,1)S(1)} %convert_element_type.307), channel_id=1, replica_groups=mesh['seq'=8,'batch'=4] {'batch'}, dimensions={0}, use_global_device_ids=true | all-gather | bytes 81920 | tf_op jit(solution)/shard_map/all_gather | solution.py:59
  115.9 13.3 %all_gather.37 = bf16[128,256]{1,0:T(8,128)(2,1)S(1)} all-gather(bf16[32,256]{1,0:T(8,128)(2,1)S(1)} %convert_element_type.301), channel_id=1, replica_groups=mesh['seq'=8,'batch'=4] {'batch'}, dimensions={0}, use_global_device_ids=true | all-gather | bytes 81920 | tf_op jit(solution)/shard_map/all_gather | solution.py:59
  129.2 14.3 %all_gather.39 = bf16[128,1024]{1,0:T(8,128)(2,1)S(1)} all-gather(bf16[32,1024]{1,0:T(8,128)(2,1)S(1)} %convert_element_type.313), channel_id=1, replica_groups=mesh['seq'=8,'batch'=4] {'batch'}, dimensions={0}, use_global_device_ids=true | all-gather | bytes 327680 | tf_op jit(solution)/shard_map/all_gather | solution.py:59
  143.6 2.1 fusion
  145.8 2.4 copy.140
  161.7 2.1 convolution_convert_fusion.2
  163.8 38.8 %reduce-scatter.12.cloned.1.call-done = bf16[128,1024]{1,0:T(8,128)(2,1)} async-done(((bf16[1024,1024]{1,0:T(8,128)(2,1)}), bf16[128,1024]{1,0:T(8,128)(2,1)}) %reduce-scatter.12.cloned.1.call-update) | async-done | bytes 262160 | tf_op jit(solution)/shard_map/reduce_scatter | solution.py:55
  204.3 1.8 multiply_convert_fusion.5
  210.4 19.0 %all_gather.41 = bf16[352,1024]{1,0:T(8,128)(2,1)} all-gather(bf16[88,1024]{1,0:T(8,128)(2,1)S(1)} %convert_element_type.318), channel_id=1, replica_groups=mesh['seq'=8,'batch'=4] {'batch'}, dimensions={0}, use_global_device_ids=true | all-gather | bytes 901120 | tf_op jit(solution)/shard_map/all_gather | solution.py:59
  229.4 4.6 all-gather.9.cloned.1.call-done
  234.0 5.8 fusion.23
  239.8 24.3 %all-gather.11.cloned.1.call-done = bf16[1024,1024]{1,0:T(8,128)(2,1)} async-done(((bf16[128,1024]{1,0:T(8,128)(2,1)}), bf16[1024,1024]{1,0:T(8,128)(2,1)}) %all-gather.11.cloned.1.call-update) | async-done | bytes 2097168 | tf_op jit(solution)/shard_map/all_gather | solution.py:51
  264.1 5.1 multiply_convert_fusion.3
  270.4 3.8 convolution_convert_fusion.3
  274.3 41.2 %reduce-scatter.16.cloned.1.call-done = bf16[128,1024]{1,0:T(8,128)(2,1)} async-done(((bf16[1024,1024]{1,0:T(8,128)(2,1)}), bf16[128,1024]{1,0:T(8,128)(2,1)}) %reduce-scatter.16.cloned.1.call-update) | async-done | bytes 262160 | tf_op jit(solution)/shard_map/reduce_scatter | solution.py:55
  315.5 1.8 fusion.53
  317.7 2.6 fusion.138
  321.8 4.8 convolution_convert_fusion.4
  326.6 2.6 copy.159
  329.2 3.6 convolution_convert_fusion.6
  333.1 15.2 %all-gather.13.cloned.1.call-done = bf16[1024,1024]{1,0:T(8,128)(2,1)} async-done(((bf16[128,1024]{1,0:T(8,128)(2,1)}), bf16[1024,1024]{1,0:T(8,128)(2,1)}) %all-gather.13.cloned.1.call-update) | async-done | bytes 2097168 | tf_op jit(solution)/shard_map/all_gather | solution.py:51
  348.3 2.5 convolution_convert_fusion.12
  365.1 3.1 fusion.31
  368.3 3.1 fusion.9
  372.6 1.7 fusion.27
  374.7 2.6 fusion.92
  378.6 1.8 copy.148
  382.3 1.7 copy.153
  389.0 2.7 fusion.28
  391.8 4.2 concatenate.44
  396.0 3.9 convolution_convert_fusion.5
  399.9 2.6 copy.155
  402.6 4.5 convolution_convert_fusion.1
  408.7 2.6 convolution_convert_fusion
  411.9 1.7 convert_element_type.356
  415.2 100.2 %all-reduce.5.cloned.1.call-done = (bf16[8,4,32,576]{3,2,1,0:T(8,128)(2,1)}, bf16[8,4,32,704]{3,2,1,0:T(8,128)(2,1)}) async-done(((bf16[8,4,32,576]{3,2,1,0:T(8,128)(2,1)}, bf16[8,4,32,704]{3,2,1,0:T(8,128)(2,1)}), (bf16[8,4,32,576]{3,2,1,0:T(8,128)(2,1)}, bf16[8,4,32,704]{3,2,1,0:T(8,128)(2,1)})) %all-reduce.5.cloned.1.call-update) | async-done | bytes 2621456
  515.3 2.4 dynamic-slice_bitcast_fusion.1
  517.7 3.7 all-to-all-start.1
  522.7 2.4 dynamic-slice_bitcast_fusion
  525.1 3.8 all-to-all-done.1
  529.0 3.5 all-to-all-start.2
  535.2 5.5 all-to-all-done.2
  543.1 15.7 %reduce-scatter.18.cloned.1.call-done = bf16[128,1024]{1,0:T(8,128)(2,1)} async-done(((bf16[1024,1024]{1,0:T(8,128)(2,1)}), bf16[128,1024]{1,0:T(8,128)(2,1)}) %reduce-scatter.18.cloned.1.call-update) | async-done | bytes 262160 | tf_op jit(solution)/shard_map/reduce_scatter | solution.py:55
  561.0 42.0 %reduce-scatter.14.cloned.1.call-done = bf16[128,1024]{1,0:T(8,128)(2,1)} async-done(((bf16[1024,1024]{1,0:T(8,128)(2,1)}), bf16[128,1024]{1,0:T(8,128)(2,1)}) %reduce-scatter.14.cloned.1.call-update) | async-done | bytes 262160 | tf_op jit(solution)/shard_map/reduce_scatter | solution.py:55
  603.1 2.8 fusion.48
  605.9 135.6 %reduce-scatter.24.cloned.1.call-done = f32[32,2]{1,0:T(8,128)} async-done(((f32[1024,2]{1,0:T(8,128)}), f32[32,2]{1,0:T(8,128)}) %reduce-scatter.24.cloned.1.call-update) | async-done | bytes 272
  (261 shorter events, 68.7 us)
Async XLA Ops:
  7.2 5.7 copy-start.39
  7.2 136.4 %all-gather.15.cloned.1.call-start = ((), (), s32[]{:S(2)}) async-start(), calls=%async_computation.19 | async-start | bytes 2359296 | tf_op jit(solution)/shard_map/all_gather | solution.py:51
  7.9 137.8 %all-gather.17.cloned.1.call-start = ((), (), s32[]{:S(2)}) async-start(), calls=%async_computation.20 | async-start | bytes 3276800 | tf_op jit(solution)/shard_map/all_gather | solution.py:103
  13.7 20.4 %copy-start.59 = (f32[32]{0:T(128)S(1)}, f32[32]{0:T(128)}, u32[]{:S(2)}) copy-start(f32[32]{0:T(128)} %param.28) | copy-start | bytes 388
  13.8 20.4 %copy-start.60 = (f32[32]{0:T(128)S(1)}, f32[32]{0:T(128)}, u32[]{:S(2)}) copy-start(f32[32]{0:T(128)} %param.20) | copy-start | bytes 388
  13.8 88.8 %copy-start.45 = (f32[32,256]{1,0:T(8,128)S(1)}, f32[32,256]{1,0:T(8,128)}, u32[]{:S(2)}) copy-start(f32[32,256]{1,0:T(8,128)} %param.25) | copy-start | bytes 98308
  13.8 88.8 %copy-start.46 = (f32[32,256]{1,0:T(8,128)S(1)}, f32[32,256]{1,0:T(8,128)}, u32[]{:S(2)}) copy-start(f32[32,256]{1,0:T(8,128)} %param.26) | copy-start | bytes 98308
  13.8 88.8 %copy-start.41 = (f32[32,1024]{1,0:T(8,128)S(1)}, f32[32,1024]{1,0:T(8,128)}, u32[]{:S(2)}) copy-start(f32[32,1024]{1,0:T(8,128)} %param.27) | copy-start | bytes 393220
  34.1 168.5 %reduce-scatter.12.cloned.1.call-start = ((), (), s32[]{:S(2)}) async-start(), calls=%async_computation.10 | async-start | bytes 2359296 | tf_op jit(solution)/shard_map/reduce_scatter | solution.py:55
  115.9 44.5 %copy-start.34 = (bf16[128,256]{1,0:T(8,128)(2,1)}, bf16[128,256]{1,0:T(8,128)(2,1)S(1)}, u32[]{:S(2)}) copy-start(bf16[128,256]{1,0:T(8,128)(2,1)S(1)} %all_gather.38) | copy-start | bytes 196612
  129.2 21.0 %copy-start.36 = (bf16[128,256]{1,0:T(8,128)(2,1)}, bf16[128,256]{1,0:T(8,128)(2,1)S(1)}, u32[]{:S(2)}) copy-start(bf16[128,256]{1,0:T(8,128)(2,1)S(1)} %all_gather.37) | copy-start | bytes 196612
  143.5 17.1 %copy-start.21 = (bf16[128,1024]{1,0:T(8,128)(2,1)}, bf16[128,1024]{1,0:T(8,128)(2,1)S(1)}, u32[]{:S(2)}) copy-start(bf16[128,1024]{1,0:T(8,128)(2,1)S(1)} %all_gather.39) | copy-start | bytes 786436
  143.5 7.8 %copy-start.54 = (f32[32]{0:T(128)}, f32[32]{0:T(128)S(1)}, u32[]{:S(2)}) copy-start(f32[32]{0:T(128)S(1)} %multiply_power_fusion) | copy-start | bytes 388
  143.6 4.6 copy-start.42
  149.8 8.2 %copy-start.10 = (bf16[1024,576]{0,1:T(8,128)(2,1)}, bf16[1024,576]{0,1:T(8,128)(2,1)S(1)}, u32[]{:S(2)}) copy-start(bf16[1024,576]{0,1:T(8,128)(2,1)S(1)} %get-tuple-element.56) | copy-start | bytes 3538948
  150.2 5.5 copy-start.16
  161.7 40.9 %copy-start.7 = (bf16[1,128,1024]{2,1,0:T(8,128)(2,1)S(1)}, bf16[1,128,1024]{2,1,0:T(8,128)(2,1)}, u32[]{:S(2)}) copy-start(bf16[1,128,1024]{2,1,0:T(8,128)(2,1)} %param.16) | copy-start | bytes 786436
  163.8 44.2 %copy-start.22 = (bf16[1,128,1024]{2,1,0:T(8,128)(2,1)S(1)}, bf16[1,128,1024]{2,1,0:T(8,128)(2,1)}, u32[]{:S(2)}) copy-start(bf16[1,128,1024]{2,1,0:T(8,128)(2,1)} %param.17) | copy-start | bytes 786436
  163.8 70.2 %all-gather.9.cloned.1.call-start = ((), (), s32[]{:S(2)}) async-start(), calls=%async_computation.11 | async-start | bytes 2359296 | tf_op jit(solution)/shard_map/all_gather | solution.py:51
  204.2 113.0 %copy-start.50 = (f32[128]{0:T(128)}, f32[128]{0:T(128)S(1)}, u32[]{:S(2)}) copy-start(f32[128]{0:T(128)S(1)} %get-tuple-element.55) | copy-start | bytes 1540
  206.0 58.1 %all-gather.11.cloned.1.call-start = ((), (), s32[]{:S(2)}) async-start(), calls=%async_computation.13 | async-start | bytes 2359296 | tf_op jit(solution)/shard_map/all_gather | solution.py:51
  209.3 106.1 %reduce-scatter.16.cloned.1.call-start = ((), (), s32[]{:S(2)}) async-start(), calls=%async_computation.14 | async-start | bytes 2359296 | tf_op jit(solution)/shard_map/reduce_scatter | solution.py:55
  264.1 6.3 copy-start.19
  274.2 41.3 %copy-start.9 = (bf16[128,1024]{1,0:T(8,128)(2,1)S(1)}, bf16[128,1024]{1,0:T(8,128)(2,1)}, u32[]{:S(2)}) copy-start(bf16[128,1024]{1,0:T(8,128)(2,1)} %reduce-scatter.12.cloned.1.call-done) | copy-start | bytes 786436
  274.2 74.1 %all-gather.13.cloned.1.call-start = ((), (), s32[]{:S(2)}) async-start(), calls=%async_computation.15 | async-start | bytes 2359296 | tf_op jit(solution)/shard_map/all_gather | solution.py:51
  320.3 91.6 %reduce-scatter.22.cloned.1.call-start = ((), (), s32[]{:S(2)}) async-start(), calls=%async_computation.18 | async-start | bytes 901120 | tf_op jit(solution)/shard_map/reduce_scatter | solution.py:63
  332.8 80.8 %reduce-scatter.20.cloned.1.call-start = ((), (), s32[]{:S(2)}) async-start(), calls=%async_computation.17 | async-start | bytes 491520 | tf_op jit(solution)/shard_map/reduce_scatter | solution.py:63
  351.4 6.8 copy-start.12
  372.6 4.7 copy-start.38
  374.4 14.6 %copy-start.6 = (bf16[1024,1024]{0,1:T(8,128)(2,1)S(1)}, bf16[1024,1024]{0,1:T(8,128)(2,1)}, u32[]{:S(2)}) copy-start(bf16[1024,1024]{0,1:T(8,128)(2,1)} %copy-done.5) | copy-start | bytes 6291460
  374.4 14.6 %copy-start.17 = (bf16[1024,256]{1,0:T(8,128)(2,1)S(1)}, bf16[1024,256]{1,0:T(8,128)(2,1)}, u32[]{:S(2)}) copy-start(bf16[1024,256]{1,0:T(8,128)(2,1)} %copy-done.16) | copy-start | bytes 1572868
  374.4 140.9 %all-reduce.5.cloned.1.call-start = ((), (), s32[]{:S(2)}) async-start(), calls=%async_computation.22 | async-start | bytes 5767168
  378.6 8.7 %copy-start.40 = (bf16[1024,32]{0,1:T(8,128)(2,1)S(1)}, bf16[1024,32]{0,1:T(8,128)(2,1)}, u32[]{:S(2)}) copy-start(bf16[1024,32]{0,1:T(8,128)(2,1)} %get-tuple-element.48) | copy-start | bytes 196612
  391.7 4.2 copy-start.26
  391.7 4.2 copy-start.43
  391.7 4.2 copy-start.53
  402.5 156.3 %reduce-scatter.18.cloned.1.call-start = ((), (), s32[]{:S(2)}) async-start(), calls=%async_computation.16 | async-start | bytes 2359296 | tf_op jit(solution)/shard_map/reduce_scatter | solution.py:55
  407.1 4.3 copy-start.62
  407.1 196.0 %reduce-scatter.14.cloned.1.call-start = ((), (), s32[]{:S(2)}) async-start(), calls=%async_computation.12 | async-start | bytes 2359296 | tf_op jit(solution)/shard_map/reduce_scatter | solution.py:55
  517.7 11.3 %all-to-all-start.1 = ((bf16[8,32,576]{2,1,0:T(8,128)(2,1)}), bf16[8,32,576]{2,1,0:T(8,128)(2,1)S(1)}, u32[]{:S(2)}, u32[]{:S(2)}) async-start(bf16[8,32,576]{2,1,0:T(8,128)(2,1)} %dynamic-slice_bitcast_fusion.1), calls=%async_computation.5 | async-start | bytes 655360 | tf_op jit(solution)/shard_map/all_to_all | solution.py:210
  529.0 11.7 %all-to-all-start.2 = ((bf16[8,32,704]{2,1,0:T(8,128)(2,1)}), bf16[8,32,704]{2,1,0:T(8,128)(2,1)S(1)}, u32[]{:S(2)}, u32[]{:S(2)}) async-start(bf16[8,32,704]{2,1,0:T(8,128)(2,1)} %dynamic-slice_bitcast_fusion), calls=%async_computation.7 | async-start | bytes 786432 | tf_op jit(solution)/shard_map/all_to_all | solution.py:210
  532.4 209.1 %reduce-scatter.24.cloned.1.call-start = ((), (), s32[]{:S(2)}) async-start(), calls=%async_computation.21 | async-start | bytes 540672
  540.8 19.1 %copy-start.47 = (f32[1024]{0:T(1024)S(1)}, f32[1024]{0:T(1024)}, u32[]{:S(2)}) copy-start(f32[1024]{0:T(1024)} %get-tuple-element.14) | copy-start | bytes 12292
  541.1 62.0 %copy-start.23 = (bf16[1,128,1024]{2,1,0:T(8,128)(2,1)S(1)}, bf16[1,128,1024]{2,1,0:T(8,128)(2,1)}, u32[]{:S(2)}) copy-start(bf16[1,128,1024]{2,1,0:T(8,128)(2,1)} %param.17) | copy-start | bytes 786436
  541.1 62.0 %copy-start.24 = (bf16[128,1024]{1,0:T(8,128)(2,1)S(1)}, bf16[128,1024]{1,0:T(8,128)(2,1)}, u32[]{:S(2)}) copy-start(bf16[128,1024]{1,0:T(8,128)(2,1)} %reduce-scatter.16.cloned.1.call-done) | copy-start | bytes 786436
  541.1 62.0 %copy-start.51 = (f32[128]{0:T(128)S(1)}, f32[128]{0:T(128)}, u32[]{:S(2)}) copy-start(f32[128]{0:T(128)} %copy-done.50) | copy-start | bytes 1540
  541.1 62.0 %copy-start.56 = (f32[128]{0:T(128)S(1)}, f32[128]{0:T(128)}, u32[]{:S(2)}) copy-start(f32[128]{0:T(128)} %get-tuple-element.54) | copy-start | bytes 1540
  541.1 62.0 %copy-start.58 = (f32[128]{0:T(128)S(1)}, f32[128]{0:T(128)}, u32[]{:S(2)}) copy-start(f32[128]{0:T(128)} %copy-done.57) | copy-start | bytes 1540
  (33 other events, 61.2 us)
Sparse Core Ops, SparseCore 0:
  9.9 35.9 all-gather.14
  47.4 55.0 all-gather.16
  163.9 38.6 reduce-scatter.11
  206.2 27.7 all-gather.8
  236.3 27.7 all-gather.10
  274.3 41.0 reduce-scatter.15
  320.5 27.7 all-gather.12
  350.6 23.0 reduce-scatter.21
  375.9 19.7 reduce-scatter.19
  402.6 112.6 all-reduce.4
  518.6 40.1 reduce-scatter.17
  561.9 41.0 reduce-scatter.13
  605.3 136.1 reduce-scatter.23

commit v2 on v1

v2 whole, which is shorter than its diff:
```python
import jax
import jax.numpy as jnp
from jax import lax
from jax.experimental import pallas as pl
from jax.experimental.pallas import tpu as pltpu
from jax.sharding import PartitionSpec as P

FF = 2816
H = 16
HD = 64
GROUPS = 2
LAT = 256
ROPE = 64
HALF = LAT // 2
PAD = 128

EPSILON = 1e-05
ROTARY_BASE = 10000.0
NEG_FILL = -1e30
BF = jnp.bfloat16
F32 = jnp.float32
MESH = pl.DeviceIdType.MESH
DMA = pltpu.SemaphoreType.DMA
VMEM = pl.BlockSpec(memory_space=pltpu.VMEM)


def mm(a, b):
    return jnp.dot(a, b, preferred_element_type=F32)


def mm_tn(a, b):
    return lax.dot_general(a, b, (((0,), (0,)), ((), ())), preferred_element_type=F32)


def mm_nt(a, b):
    return lax.dot_general(a, b, (((1,), (1,)), ((), ())), preferred_element_type=F32)


def rms(v, g):
    inv = lax.rsqrt(jnp.mean(v * v, -1, keepdims=True) + EPSILON)
    return inv, v * inv * g


def rms_grad(v, inv, g, dn):
    scaled = dn * g
    back = inv * scaled - v * (inv * inv * inv) * jnp.mean(scaled * v, -1, keepdims=True)
    return back, jnp.sum(dn * v * inv, 0, keepdims=True)


def rotate(v, cosine, sine):
    half = v.shape[-1] // 2
    lo, hi = v[..., :half], v[..., half:]
    return jnp.concatenate([lo * cosine - hi * sine, lo * sine + hi * cosine], -1)


def last(mask):
    return mask.bit_length() - 1


def aligned(start, size):
    return pl.ds(pl.multiple_of(start, size), size)


class Place:
    def __init__(self, ns, nb):
        self.ns, self.nb, self.nc = ns, nb, ns // 2
        self.dims = last(self.nc)
        self.me = lax.axis_index("seq")
        self.bat = lax.axis_index("batch")
        self.core = lax.rem(self.me, 2)
        self.chip = self.me // 2
        self.sib = self.chip * 2 + 1 - self.core

    def across(self, mask, core):
        spot = self.chip
        for j in range(self.dims):
            if mask >> j & 1:
                step = core * (1 << j) + (1 - core) * (1 << (self.dims - 1 - j))
                spot = spot + step - 2 * step * lax.rem(spot // step, 2)
        return spot * 2 + core

    def at(self, mask):
        return self.across(mask, self.core)

    def sib_at(self, mask):
        return self.across(mask, 1 - self.core)

    def seq(self, src, dst, send, recv, to):
        return pltpu.make_async_remote_copy(src, dst, send, recv, device_id={"seq": to}, device_id_type=MESH)

    def batch(self, src, dst, send, recv, to):
        return pltpu.make_async_remote_copy(src, dst, send, recv, device_id={"batch": to}, device_id_type=MESH)

    def barrier(self, all_seq, all_batch):
        sem = pltpu.get_barrier_semaphore()
        if all_seq:
            peers = [lax.rem(self.me + t, self.ns) for t in range(1, self.ns)]
        else:
            peers = [self.sib] + [self.at(1 << j) for j in range(self.dims)]
        for to in peers:
            pl.semaphore_signal(sem, 1, device_id={"seq": to}, device_id_type=MESH)
        count = len(peers)
        if all_batch:
            for t in range(1, self.nb):
                to = lax.rem(self.bat + t, self.nb)
                pl.semaphore_signal(sem, 1, device_id={"batch": to}, device_id_type=MESH)
            pl.semaphore_wait(sem, count + self.nb - 1)
            return

        @pl.when(self.bat > 0)
        def _():
            pl.semaphore_signal(sem, 1, device_id={"batch": self.bat - 1}, device_id_type=MESH)

        @pl.when(self.bat < self.nb - 1)
        def _():
            pl.semaphore_signal(sem, 1, device_id={"batch": self.bat + 1}, device_id_type=MESH)

        up = (self.bat > 0).astype(jnp.int32)
        down = (self.bat < self.nb - 1).astype(jnp.int32)
        pl.semaphore_wait(sem, count + up + down)


class Gather:
    def __init__(self, place, src, out, chunks, sems):
        self.place, self.src, self.out, self.chunks = place, src, out, chunks
        self.rows = src.shape[0]
        self.send, self.recv, self.sib_send, self.sib_recv = sems

    @staticmethod
    def sems(ns, chunks):
        nc = ns // 2
        hops, blocks = max(nc - 1, 1) * chunks, nc * chunks
        return [DMA((hops,)), DMA((hops,)), DMA((blocks,)), DMA((blocks,))]

    def slot(self, dev, ch):
        n = self.rows // self.chunks
        return self.out.at[pl.ds(pl.multiple_of(dev * self.rows + ch * n, n), n)]

    def block(self, mask, ch):
        n = self.rows // self.chunks
        if mask == 0:
            return self.src.at[pl.ds(ch * n, n)]
        return self.slot(self.place.at(mask), ch)

    def sends(self, mask, ch):
        place, copies = self.place, []
        for j in range(last(mask) + 1, place.dims):
            i = ((mask | 1 << j) - 1) * self.chunks + ch
            copies.append(
                place.seq(
                    self.block(mask, ch),
                    self.slot(place.at(mask), ch),
                    self.send.at[i],
                    self.recv.at[i],
                    place.at(1 << j),
                )
            )
        i = mask * self.chunks + ch
        copies.append(
            place.seq(
                self.block(mask, ch), self.slot(place.at(mask), ch), self.sib_send.at[i], self.sib_recv.at[i], place.sib
            )
        )
        return copies

    def start(self):
        for ch in range(self.chunks):
            for copy in self.sends(0, ch):
                copy.start()

    def relay(self, masks=None):
        place = self.place
        for mask in masks or range(1, place.nc):
            for ch in range(self.chunks):
                i = (mask - 1) * self.chunks + ch
                spot = self.slot(place.at(mask), ch)
                place.seq(spot, spot, self.send.at[i], self.recv.at[i], place.at(1 << last(mask))).wait_recv()
                for copy in self.sends(mask, ch):
                    copy.start()

    def finish(self):
        place = self.place
        for mask in range(place.nc):
            for ch in range(self.chunks):
                for copy in self.sends(mask, ch):
                    copy.wait_send()
                i = mask * self.chunks + ch
                spot = self.slot(place.sib_at(mask), ch)
                place.seq(spot, spot, self.sib_send.at[i], self.sib_recv.at[i], place.sib).wait_recv()


class Scatter:
    def __init__(self, place, part, bufs, sems):
        self.place, self.part = place, part
        self.acc, self.land, self.sib_land = bufs
        self.send, self.recv, self.sib_send, self.sib_recv = sems
        self.rows = part.shape[0] // place.ns

    @staticmethod
    def sems(ns):
        nc = ns // 2
        return [DMA((max(nc - 1, 1),)), DMA((max(nc - 1, 1),)), DMA((nc,)), DMA((nc,))]

    @staticmethod
    def bufs(ns, rows, width):
        return [pltpu.VMEM((ns // 2, rows, width), BF)] * 3

    def own(self, dev):
        return self.part.at[aligned(dev * self.rows, self.rows)]

    def sibling(self, mask):
        place = self.place
        return place.seq(
            self.own(place.sib_at(mask)),
            self.sib_land.at[mask],
            self.sib_send.at[mask],
            self.sib_recv.at[mask],
            place.sib,
        )

    def hop(self, mask):
        place = self.place
        return place.seq(
            self.acc.at[mask],
            self.land.at[mask],
            self.send.at[mask - 1],
            self.recv.at[mask - 1],
            place.at(1 << last(mask)),
        )

    def start(self):
        for mask in reversed(range(self.place.nc)):
            self.sibling(mask).start()

    def step(self, mask):
        place = self.place
        self.sibling(mask).wait_recv()
        value = self.own(place.at(mask))[...].astype(F32) + self.sib_land[mask].astype(F32)
        for j in reversed(range(last(mask) + 1, place.dims)):
            self.hop(mask | 1 << j).wait_recv()
            value = value + self.land[mask | 1 << j].astype(F32)
        if mask:
            self.acc[mask] = value.astype(BF)
            self.hop(mask).start()
        return value

    def total(self):
        for mask in reversed(range(1, self.place.nc)):
            self.step(mask)
        return self.step(0)

    def finish(self):
        for mask in range(self.place.nc):
            self.sibling(mask).wait_send()
            if mask:
                self.hop(mask).wait_send()


class Line:
    def __init__(self, place, slots, sems):
        self.place, self.slots = place, slots
        self.send, self.recv = sems

    @staticmethod
    def sems(nb, parts):
        return [DMA((2 * nb * parts,)), DMA((2 * nb * parts,))]

    def copy(self, up, d, i):
        place = self.place
        block = place.bat - d if up else place.bat + d
        to = place.bat + 1 if up else place.bat - 1
        ref = self.slots[i](block)
        at = (int(up) * place.nb + d) * len(self.slots) + i
        return place.batch(ref, ref, self.send.at[at], self.recv.at[at], to)

    def sends(self, up, d):
        bat, nb = self.place.bat, self.place.nb
        return (bat - d >= 0) & (bat + 1 < nb) if up else (bat + d < nb) & (bat >= 1)

    def start(self, d, parts):
        for up in (True, False):

            @pl.when(self.sends(up, d))
            def _(up=up):
                for i in parts:
                    self.copy(up, d, i).start()

    def came(self, up, d):
        return self.place.bat - d >= 0 if up else self.place.bat + d < self.place.nb

    def relay(self, d, parts, then=None):
        bat, nb = self.place.bat, self.place.nb
        for up in (True, False):

            @pl.when(self.came(up, d))
            def _(up=up):
                for i in parts:
                    block = bat - d if up else bat + d
                    ref = self.slots[i](block)
                    at = (int(up) * nb + d - 1) * len(self.slots) + i
                    self.place.batch(ref, ref, self.send.at[at], self.recv.at[at], bat).wait_recv()
                    if d < nb - 1:

                        @pl.when(self.sends(up, d))
                        def _():
                            self.copy(up, d, i).start()

                    if then:
                        then(block, up, i)

    def finish(self, parts):
        for d in range(self.place.nb - 1):
            for up in (True, False):

                @pl.when(self.sends(up, d))
                def _(up=up, d=d):
                    for i in parts:
                        self.copy(up, d, i).wait_send()


class LineSum:
    def __init__(self, place, parts, bufs, sems):
        self.place, self.parts = place, parts
        self.bufs = [bufs[4 * i : 4 * i + 4] for i in range(len(parts))]
        self.send, self.recv = sems

    @staticmethod
    def sems(nb, parts):
        return [DMA((2 * nb * parts,)), DMA((2 * nb * parts,))]

    @staticmethod
    def scratch(nb, shapes):
        return [pltpu.VMEM((nb - 1,) + shape, BF) for shape in shapes for _ in range(4)]

    def copy(self, up, d, i, first):
        place = self.place
        land, acc = self.bufs[i][:2] if up else self.bufs[i][2:]
        to = place.bat + 1 if up else place.bat - 1
        dest = place.bat + d if up else place.bat - d
        src = self.parts[i](dest) if first else acc.at[d - 1]
        at = (int(up) * place.nb + d) * len(self.parts) + i
        return place.batch(src, land.at[d - 1], self.send.at[at], self.recv.at[at], to)

    def arrived(self, up, d, i):
        place = self.place
        land = self.bufs[i][0 if up else 2]
        at = (int(up) * place.nb + d + 1) * len(self.parts) + i
        place.batch(land.at[d], land.at[d], self.send.at[at], self.recv.at[at], place.bat).wait_recv()
        return land[d].astype(F32)

    def edge(self, up):
        return self.place.bat == 0 if up else self.place.bat == self.place.nb - 1

    def inside(self, up, d):
        return self.place.bat + d < self.place.nb if up else self.place.bat - d >= 0

    def start(self):
        for d in reversed(range(1, self.place.nb)):
            for up in (True, False):

                @pl.when(self.edge(up))
                def _(up=up, d=d):
                    for i in range(len(self.parts)):
                        self.copy(up, d, i, True).start()

    def stage(self, d):
        for up in (True, False):

            @pl.when(self.inside(up, d) & jnp.logical_not(self.edge(up)))
            def _(up=up):
                for i in range(len(self.parts)):
                    dest = self.place.bat + d if up else self.place.bat - d
                    acc = self.bufs[i][1 if up else 3]
                    acc[d - 1] = (self.parts[i](dest)[...].astype(F32) + self.arrived(up, d, i)).astype(BF)
                    self.copy(up, d, i, False).start()

    def total(self, outs):
        for i, out in enumerate(outs):
            out[...] = self.parts[i](self.place.bat)[...].astype(out.dtype)
            for up in (True, False):

                @pl.when(jnp.logical_not(self.edge(up)))
                def _(up=up):
                    out[...] = (out[...].astype(F32) + self.arrived(up, 0, i)).astype(out.dtype)

    def finish(self):
        for d in range(1, self.place.nb):
            for up in (True, False):

                @pl.when(self.inside(up, d) & self.edge(up))
                def _(up=up, d=d):
                    for i in range(len(self.parts)):
                        self.copy(up, d, i, True).wait_send()

                @pl.when(self.inside(up, d) & jnp.logical_not(self.edge(up)))
                def _(up=up, d=d):
                    for i in range(len(self.parts)):
                        self.copy(up, d, i, False).wait_send()


class Exchange:
    def __init__(self, place, pieces, slots, sems):
        self.place, self.pieces, self.slots = place, pieces, slots
        self.send, self.recv = sems

    @staticmethod
    def sems(ns, parts):
        return [DMA((ns * parts,)), DMA((ns * parts,))]

    def copy(self, t, i):
        place = self.place
        to = lax.rem(place.me + t, place.ns)
        at = t * len(self.pieces) + i
        src, dst = self.pieces[i](to), self.slots[i](place.me, to)
        if t == 0:
            return pltpu.make_async_copy(src, dst, self.recv.at[at])
        return place.seq(src, dst, self.send.at[at], self.recv.at[at], to)

    def start(self):
        for t in range(self.place.ns):
            for i in range(len(self.pieces)):
                self.copy(t, i).start()

    def arrive(self):
        place = self.place
        for t in range(place.ns):
            for i in range(len(self.pieces)):
                if t == 0:
                    self.copy(0, i).wait()
                    continue
                at = t * len(self.pieces) + i
                spot = self.slots[i](lax.rem(place.me + place.ns - t, place.ns), place.me)
                place.seq(spot, spot, self.send.at[at], self.recv.at[at], place.sib).wait_recv()

    def finish(self):
        for t in range(1, self.place.ns):
            for i in range(len(self.pieces)):
                self.copy(t, i).wait_send()


def take(refs, counts):
    out, at = [], 0
    for n in counts:
        out.append(refs[at : at + n])
        at += n
    return out


def comm_call(body, out_shape, scratch, cid, *args):
    return pl.pallas_call(
        body,
        out_shape=out_shape,
        in_specs=[VMEM] * len(args),
        out_specs=[VMEM] * len(out_shape),
        scratch_shapes=scratch,
        compiler_params=pltpu.CompilerParams(
            collective_id=cid, has_side_effects=True, vmem_limit_bytes=60 << 20
        ),
    )(*args)


def sds(shape, dtype):
    return jax.ShapeDtypeStruct(tuple(shape), dtype)


def fetch(ns, nb, x, dy, wide_a, wide_f, head_rows, chunks=4):
    rows, width = x.shape
    shard, aw = wide_a.shape[1:]
    qk = aw - HALF
    full = qk + LAT

    def body(x, dy, wa, wf, hr, x_all, dy_all, a_out, f_out, h_out, *rest):
        gx, gd, ea, ef, zl, local, sib = take(rest, (4, 4, 2, 2, 2, 1, 2))
        place = Place(ns, nb)
        local = local[0]
        mine = aligned(place.me * rows, rows)
        copies = [
            pltpu.make_async_copy(x, x_all.at[mine], local.at[0]),
            pltpu.make_async_copy(dy, dy_all.at[mine], local.at[1]),
            pltpu.make_async_copy(hr, h_out.at[place.bat], local.at[2]),
        ]
        for copy in copies:
            copy.start()
        place.barrier(True, False)

        def half(core):
            return pl.ds(pl.multiple_of(qk + HALF * core, HALF), HALF)

        cols = Exchange(
            place,
            [lambda to: wa.at[to, :, pl.ds(0, qk)], lambda to: wa.at[to, :, pl.ds(qk, HALF)]],
            [
                lambda frm, to: a_out.at[frm, place.bat, :, pl.ds(0, qk)],
                lambda frm, to: a_out.at[frm, place.bat, :, half(lax.rem(to, 2))],
            ],
            ea,
        )
        ffn = Exchange(place, [lambda to: wf.at[to]], [lambda frm, to: f_out.at[frm]], ef)
        along = Line(
            place,
            [
                lambda b: h_out.at[b],
                lambda b: a_out.at[:, b, :, pl.ds(0, qk)],
                lambda b: a_out.at[:, b, :, half(place.core)],
            ],
            zl,
        )

        def to_sibling(b, i):
            ref = a_out.at[:, b, :, half(place.core)]
            return place.seq(ref, ref, sib[0].at[i], sib[1].at[i], place.sib)

        xs, ds = Gather(place, x, x_all, chunks, gx), Gather(place, dy, dy_all, chunks, gd)
        cols.start()
        copies[2].wait()
        along.start(0, [0])
        xs.start()
        ffn.start()
        ds.start()
        cols.arrive()
        along.start(0, [1, 2])
        to_sibling(place.bat, 0).start()
        xs.relay()

        def then(b, up, d):
            to_sibling(b, d if up else nb - 1 + d).start()

        for d in range(1, nb):
            along.relay(d, [0])
        for d in range(1, nb):
            along.relay(d, [1])
            along.relay(d, [2], lambda b, up, i, d=d: then(b, up, d))
            if d == 1:
                ds.relay()
        ffn.arrive()
        xs.finish()
        ds.finish()
        cols.finish()
        ffn.finish()
        along.finish([0, 1, 2])

        def other(b, i):
            ref = a_out.at[:, b, :, half(1 - place.core)]
            place.seq(ref, ref, sib[0].at[i], sib[1].at[i], place.sib).wait_recv()

        to_sibling(place.bat, 0).wait_send()
        other(place.bat, 0)
        for d in range(1, nb):
            for up in (True, False):

                @pl.when(along.came(up, d))
                def _(up=up, d=d):
                    b = place.bat - d if up else place.bat + d
                    i = d if up else nb - 1 + d
                    to_sibling(b, i).wait_send()
                    other(b, i)

        copies[0].wait()
        copies[1].wait()

    scratch = (
        Gather.sems(ns, chunks)
        + Gather.sems(ns, chunks)
        + Exchange.sems(ns, 2)
        + Exchange.sems(ns, 1)
        + Line.sems(nb, 3)
        + [DMA((3,)), DMA((2 * nb,)), DMA((2 * nb,))]
    )
    return comm_call(
        body,
        [
            sds((ns * rows, width), BF),
            sds((ns * rows, width), BF),
            sds((ns, nb, shard, full), BF),
            sds(wide_f.shape, BF),
            sds((nb,) + head_rows.shape, BF),
        ],
        scratch,
        1,
        x,
        dy,
        wide_a,
        wide_f,
        head_rows,
    )


def turn_forward(ns, nb, part, x, gain, wide_f, down, chunks=4):
    rows, width = x.shape

    def body(part, x, gain, wf, dn, hres, b_all, f_out, d_out, own, *rest):
        bufs, rs, gs, zl, local = take(rest, (3, 4, 4, 2, 1))
        place = Place(ns, nb)
        local = local[0]
        copies = [
            pltpu.make_async_copy(wf, f_out.at[:, place.bat], local.at[0]),
            pltpu.make_async_copy(dn, d_out.at[place.bat], local.at[1]),
        ]
        for copy in copies:
            copy.start()
        place.barrier(False, False)
        sums = Scatter(place, part, bufs, rs)
        sums.start()
        along = Line(place, [lambda b: f_out.at[:, b], lambda b: d_out.at[b]], zl)
        for copy in copies:
            copy.wait()
        along.start(0, [0, 1])
        value = x[...].astype(F32) + sums.total()
        hres[...] = value
        own[...] = rms(value, gain[...])[1].astype(BF)
        spread = Gather(place, own, b_all, chunks, gs)
        spread.start()
        mine = pltpu.make_async_copy(own, b_all.at[aligned(place.me * rows, rows)], local.at[2])
        mine.start()
        along.relay(1, [0, 1])
        spread.relay()
        for d in range(2, nb):
            along.relay(d, [0, 1])
        spread.finish()
        sums.finish()
        along.finish([0, 1])
        mine.wait()

    scratch = (
        [pltpu.VMEM((rows, width), BF)]
        + Scatter.bufs(ns, rows, width)
        + Scatter.sems(ns)
        + Gather.sems(ns, chunks)
        + Line.sems(nb, 2)
        + [DMA((3,))]
    )
    return comm_call(
        body,
        [
            sds((rows, width), F32),
            sds((ns * rows, width), BF),
            sds((ns, nb) + wide_f.shape[1:], BF),
            sds((nb,) + down.shape, BF),
        ],
        scratch,
        2,
        part,
        x,
        gain,
        wide_f,
        down,
    )


def turn_back(ns, nb, part, gy, hres, gain, g_wide, g_down, chunks=4):
    rows, width = gy.shape

    def body(part, gy, hres, gain, gw, gd, dres, dat_all, gg, w_out, d_out, own, *rest):
        bufs, rs, gs, zb, zs, local = take(rest, (3, 4, 4, 8, 2, 1))
        place = Place(ns, nb)
        local = local[0]
        place.barrier(False, False)
        sums = Scatter(place, part, bufs, rs)
        sums.start()
        along = LineSum(place, [lambda b: gw.at[:, b], lambda b: gd.at[b]], zb, zs)
        along.start()
        db = sums.total()
        value = hres[...]
        inv = rms(value, gain[...])[0]
        back, gg[...] = rms_grad(value, inv, gain[...], db)
        value = gy[...] + back
        dres[...] = value
        own[...] = value.astype(BF)
        spread = Gather(place, own, dat_all, chunks, gs)
        spread.start()
        mine = pltpu.make_async_copy(own, dat_all.at[aligned(place.me * rows, rows)], local.at[0])
        mine.start()
        for d in reversed(range(1, nb - 1)):
            if d == nb - 3:
                spread.relay()
            along.stage(d)
        along.total([w_out, d_out])
        spread.finish()
        sums.finish()
        along.finish()
        mine.wait()

    scratch = (
        [pltpu.VMEM((rows, width), BF)]
        + Scatter.bufs(ns, rows, width)
        + Scatter.sems(ns)
        + Gather.sems(ns, chunks)
        + LineSum.scratch(nb, [(ns,) + g_wide.shape[2:], g_down.shape[1:]])
        + LineSum.sems(nb, 2)
        + [DMA((1,))]
    )
    return comm_call(
        body,
        [
            sds((rows, width), F32),
            sds((ns * rows, width), BF),
            sds((1, width), F32),
            sds((ns,) + g_wide.shape[2:], BF),
            sds(g_down.shape[1:], F32),
        ],
        scratch,
        3,
        part,
        gy,
        hres,
        gain,
        g_wide,
        g_down,
    )


def settle(ns, nb, part, part_y, x, hres, dres, gain, gg_f, g_cols, g_rows, g_wide):
    rows, width = x.shape

    def body(part, py, x, hres, dres, gain, ggf, gc, gr, gw, dx, y, gg, c_out, r_out, w_out, *rest):
        c_sum, g_own, g_seq, g_bat = rest[:4]
        ba, ra, by, ry, zb, zs, ec, ew, gs, gb = take(rest[4:], (3, 4, 3, 4, 8, 2, 2, 2, 2, 2))
        place = Place(ns, nb)
        place.barrier(True, True)
        sums, outs = Scatter(place, part, ba, ra), Scatter(place, py, by, ry)
        sums.start()
        along = LineSum(place, [lambda b: gc.at[:, b], lambda b: gr.at[b]], zb, zs)
        along.start()
        outs.start()
        wide = Exchange(place, [lambda to: gw.at[to]], [lambda frm, to: w_out.at[frm]], ew)
        da = sums.total()
        wide.start()
        value = x[...].astype(F32)
        inv = rms(value, gain[...])[0]
        back, gg_a = rms_grad(value, inv, gain[...], da)
        dx[...] = dres[...] + back
        g_own[pl.ds(0, 1)] = gg_a
        g_own[pl.ds(1, 1)] = ggf[...]
        gains = Exchange(place, [lambda to: g_own], [lambda frm, to: g_seq.at[frm]], gs)
        gains.start()
        stages = list(reversed(range(1, nb - 1)))
        for d in stages[:1]:
            along.stage(d)
        y[...] = (hres[...] + outs.total()).astype(BF)
        for d in stages[1:]:
            along.stage(d)
        gains.arrive()
        gains.finish()
        g_own[...] = jnp.sum(g_seq[...], 0)

        def gain_copy(t):
            to = lax.rem(place.bat + t, nb)
            return place.batch(g_own, g_bat.at[place.bat], gb[0].at[t], gb[1].at[t], to)

        for t in range(1, nb):
            gain_copy(t).start()
        along.total([c_sum, r_out])
        cols = Exchange(place, [lambda to: c_sum.at[to]], [lambda frm, to: c_out.at[frm]], ec)
        cols.start()
        g_bat[place.bat] = g_own[...]
        for t in range(1, nb):
            spot = g_bat.at[lax.rem(place.bat + nb - t, nb)]
            place.batch(spot, spot, gb[0].at[t], gb[1].at[t], place.bat).wait_recv()
        gg[...] = jnp.sum(g_bat[...], 0)
        wide.arrive()
        cols.arrive()
        for t in range(1, nb):
            gain_copy(t).wait_send()
        sums.finish()
        outs.finish()
        along.finish()
        wide.finish()
        cols.finish()

    block = (ns,) + g_cols.shape[2:]
    scratch = (
        [
            pltpu.VMEM(block, BF),
            pltpu.VMEM((2, width), F32),
            pltpu.VMEM((ns, 2, width), F32),
            pltpu.VMEM((nb, 2, width), F32),
        ]
        + Scatter.bufs(ns, rows, width)
        + Scatter.sems(ns)
        + Scatter.bufs(ns, rows, width)
        + Scatter.sems(ns)
        + LineSum.scratch(nb, [block, g_rows.shape[1:]])
        + LineSum.sems(nb, 2)
        + Exchange.sems(ns, 1)
        + Exchange.sems(ns, 1)
        + Exchange.sems(ns, 1)
        + [DMA((nb,)), DMA((nb,))]
    )
    return comm_call(
        body,
        [
            sds((rows, width), F32),
            sds((rows, width), BF),
            sds((2, width), F32),
            sds(block, BF),
            sds(g_rows.shape[1:], F32),
            sds(g_wide.shape, BF),
        ],
        scratch,
        4,
        part,
        part_y,
        x,
        hres,
        dres,
        gain,
        gg_f,
        g_cols,
        g_rows,
        g_wide,
    )


def local(
    tokens,
    out_grad,
    group_id,
    group_weight,
    gain_attn,
    w_query,
    w_qrope,
    w_latent,
    w_krope,
    w_ukey,
    w_uval,
    w_out,
    gain_ffn,
    w_gate,
    w_up,
    w_down,
):
    ns, nb = lax.axis_size("seq"), lax.axis_size("batch")
    me, bat = lax.axis_index("seq"), lax.axis_index("batch")
    seq_count, rows, width = tokens.shape
    shard = w_query.shape[0]
    length = rows * ns
    hl, fl = H // ns, FF // ns
    qw, rw = hl * HD, hl * ROPE
    scaling = (HD + ROPE) ** (-0.5)

    x = tokens.reshape(rows, width)
    domains = jnp.arange(group_weight.shape[0])
    seq_weight = jnp.sum(jnp.where(group_id[:, None] == domains[None, :], group_weight[None, :], 0.0), -1)
    gy = (out_grad.astype(F32) * seq_weight[:, None, None]).reshape(rows, width)

    def columns(w, blocks):
        return w.astype(BF).reshape(shard, blocks, -1).transpose(1, 0, 2)

    extra = jnp.concatenate(
        [
            w_krope.astype(BF),
            gain_attn.astype(BF)[:, None],
            gain_ffn.astype(BF)[:, None],
            jnp.zeros((shard, PAD - ROPE - 2), BF),
        ],
        1,
    )
    extra = jnp.broadcast_to(extra[None], (ns, shard, PAD))
    lat = columns(w_latent, GROUPS * 2).reshape(GROUPS, 1, 2, shard, HALF)
    lat = jnp.broadcast_to(lat, (GROUPS, ns // GROUPS // 2, 2, shard, HALF)).reshape(ns, shard, HALF)
    wide_a = jnp.concatenate([columns(w_query, ns), columns(w_qrope, ns), extra, lat], -1)
    wide_f = jnp.concatenate([columns(w_gate, ns), columns(w_up, ns)], -1)
    head_rows = jnp.concatenate([w_ukey, w_uval, w_out], 1).astype(BF)

    x_all, dy_all, acols, fcols, hrows = fetch(ns, nb, x, gy.astype(BF), wide_a, wide_f, head_rows)
    kr_at = qw + rw
    lat_at = kr_at + PAD
    full = lat_at + LAT
    wcat = acols.reshape(width, full)
    gains = wcat[:, kr_at + ROPE : kr_at + ROPE + 2].astype(F32).T
    gain_a, gain_f = gains[:1], gains[1:]
    hrows = hrows.reshape(nb * shard, -1)
    ukey, uval, wout = hrows[:, :LAT], hrows[:, LAT : 2 * LAT], hrows[:, 2 * LAT :]

    position = jnp.arange(length).astype(F32)
    freq = ROTARY_BASE ** (-jnp.arange(ROPE // 2).astype(F32) * 2.0 / ROPE)
    angles = position[:, None] * freq
    cosine, sine = jnp.cos(angles), jnp.sin(angles)

    a_all = rms(x_all.astype(F32), gain_a)[1].astype(BF)
    qkv = mm(a_all, wcat)
    q = qkv[:, :qw].astype(BF)
    qr = rotate(qkv[:, qw : qw + rw].reshape(length, hl, ROPE), cosine[:, None], sine[:, None]).astype(BF)
    c = qkv[:, lat_at:].astype(BF)
    kr = rotate(qkv[:, kr_at : kr_at + ROPE], cosine, sine).astype(BF)
    causal = jnp.arange(length)[None, :] <= jnp.arange(length)[:, None]

    keep = []
    outs = []
    for h in range(hl):
        uh = ukey[h * HD : (h + 1) * HD]
        vh = uval[h * HD : (h + 1) * HD]
        ql = mm(q[:, h * HD : (h + 1) * HD], uh).astype(BF)
        sc = (mm_nt(ql, c) + mm_nt(qr[:, h], kr)) * scaling
        sc = jnp.where(causal, sc, NEG_FILL)
        top = jnp.max(sc, -1, keepdims=True)
        e = jnp.exp(sc - top)
        total = jnp.sum(e, -1, keepdims=True)
        ol = mm(e.astype(BF), c) / total
        olb = ol.astype(BF)
        outs.append(mm_nt(olb, vh).astype(BF))
        keep.append((ql, ol, olb, top + jnp.log(total)))
    o = jnp.concatenate(outs, -1)
    hres, b_all, fcols, drows = turn_forward(
        ns, nb, mm(o, wout).astype(BF), x, gain_f, fcols, w_down.astype(BF)
    )
    wgu = fcols.reshape(width, 2 * fl)
    wdown = drows.reshape(fl, width)
    gu = mm(b_all, wgu)
    gate, up = gu[:, :fl], gu[:, fl:]
    sig = jax.nn.sigmoid(gate)
    act = gate * sig
    hid = (act * up).astype(BF)
    part_y = mm(hid, wdown).astype(BF)

    dhid = mm_nt(dy_all, wdown)
    dgate = (dhid * up * sig * (1.0 + gate * (1.0 - sig))).astype(BF)
    dup = (dhid * act).astype(BF)
    dgu = jnp.concatenate([dgate, dup], -1)
    g_down = mm_tn(hid, dy_all).astype(BF).reshape(nb, fl // nb, width)
    g_gu = mm_tn(b_all, dgu).astype(BF).reshape(ns, nb, shard, 2 * fl)
    dres, dat_all, gg_f, g_gu, p_down = turn_back(
        ns, nb, mm_nt(dgu, wgu).astype(BF), gy, hres, gain_f, g_gu, g_down
    )
    g_out = mm_tn(o, dat_all)
    do = mm_nt(dat_all, wout).astype(BF)

    dqs, dqps, g_uk, g_uv = [], [], [], []
    dc = jnp.zeros((length, LAT), F32)
    dkr = jnp.zeros((length, ROPE), F32)
    for h in range(hl):
        ql, ol, olb, lse = keep[h]
        uh = ukey[h * HD : (h + 1) * HD]
        vh = uval[h * HD : (h + 1) * HD]
        doh = do[:, h * HD : (h + 1) * HD]
        g_uv.append(mm_tn(doh, olb))
        dol = mm(doh, vh).astype(BF)
        delta = jnp.sum(dol.astype(F32) * ol, -1, keepdims=True)
        sc = (mm_nt(ql, c) + mm_nt(qr[:, h], kr)) * scaling
        p = jnp.exp(jnp.where(causal, sc, NEG_FILL) - lse)
        ds = (p * (mm_nt(dol, c) - delta)).astype(BF)
        dql = (scaling * mm(ds, c)).astype(BF)
        dqps.append(rotate(scaling * mm(ds, kr), cosine, -sine).astype(BF))
        dkr = dkr + scaling * mm_tn(ds, qr[:, h])
        dc = dc + mm_tn(p.astype(BF), dol) + scaling * mm_tn(ds, ql)
        g_uk.append(mm_tn(q[:, h * HD : (h + 1) * HD], dql))
        dqs.append(mm_nt(dql, uh).astype(BF))
    dkp = rotate(dkr, cosine, -sine).astype(BF)
    gcat = jnp.concatenate(dqs + dqps + [dkp, jnp.zeros((length, PAD - ROPE), BF), dc.astype(BF)], -1)
    g_cat = mm_tn(a_all, gcat).astype(BF).reshape(ns, nb, shard, full)
    g_head = jnp.concatenate([jnp.concatenate(g_uk, 0), jnp.concatenate(g_uv, 0), g_out], -1)
    g_head = g_head.astype(BF).reshape(nb, shard, -1)
    dx, y, gg, r_cat, p_head, r_gu = settle(
        ns, nb, mm_nt(gcat, wcat).astype(BF), part_y, x, hres, dres, gain_a, gg_f, g_cat, g_head, g_gu
    )

    def spread(v):
        return v.transpose(1, 0, 2).reshape(shard, -1).astype(F32)

    group = ns // GROUPS
    p_latent = r_cat[:, :, lat_at:].astype(F32).reshape(GROUPS, group, shard, LAT).sum(1)
    gg = lax.dynamic_slice(gg, (0, (me * nb + bat) * shard), (2, shard))
    return (
        y.reshape(seq_count, rows, width),
        dx.reshape(seq_count, rows, width),
        gg[0],
        spread(r_cat[:, :, :qw]),
        spread(r_cat[:, :, qw : qw + rw]),
        spread(p_latent),
        r_cat[:, :, kr_at : kr_at + ROPE].astype(F32).sum(0),
        p_head[:, :LAT],
        p_head[:, LAT : 2 * LAT],
        p_head[:, 2 * LAT :],
        gg[1],
        spread(r_gu[:, :, :fl]),
        spread(r_gu[:, :, fl:]),
        p_down,
    )


def solution(mesh):
    token, row, flat = P("batch", "seq", None), P(("seq", "batch"), None), P(("seq", "batch"))
    return jax.shard_map(
        local,
        mesh=mesh,
        in_specs=(token, token, P("batch"), P(), flat, row, row, row, row, row, row, row, flat, row, row, row),
        out_specs=(token, token, flat, row, row, row, row, row, row, row, flat, row, row, row),
        check_vma=False,
    )
```

time: 755 us -> 301 us (0.40)
  waiting for transfers between devices: 428 us -> 0 us
  Pallas kernels: 0 us -> 197 us
  blocking collectives: 147 us -> 0 us
  local copies, waits for them, and re-layouts: 50.5 us -> 31.3 us
  matrix products: 69.9 us -> 51.7 us
  other arithmetic: 31 us -> 15.9 us
  between operations: 15.8 us -> 2.55 us
  starting transfers between devices: 8.11 us -> 0 us
    unnamed x15 -> x0, waiting for transfers between devices: 237 us -> none
    pallas_call x0 -> x4, Pallas kernels: none -> 197 us  [comm_call(): pl.pallas_call(body, out_shape=out_shape, in_specs=[VMEM] * len(args), ou...]
    reduce_scatter x6 -> x0, waiting for transfers between devices: 138 us -> none  [the longest x4 138 us: seq_sum(): lax.psum_scatter(v.astype(BF), 'seq', scatter_dimension=0, tiled=True)]
    all_gather x5 -> x0, blocking collectives: 128 us -> none  [the longest x1 68.3 us: local(): lax.all_gather(jnp.stack([gain_attn, gain_ffn]).astype(BF), ('seq', 'batc...]
    all_gather x5 -> x0, waiting for transfers between devices: 44.2 us -> none  [the longest x4 44.1 us: seq_gather(): return lax.all_gather(v, 'seq', axis=0, tiled=True)]
    all_to_all x1 -> x0, blocking collectives: 18.9 us -> none  [local(): got = lax.all_to_all(send, 'seq', 0, 0)]
    dot_general x14, matrix products: 26.7 us -> 14.5 us  [mm_tn(): lax.dot_general(a, b, (((0,), (0,)), ((), ())), preferred_element_type=F32)]
    all_to_all x2 -> x0, waiting for transfers between devices: 9.33 us -> none  [wide_sum(): return lax.all_to_all(part, 'seq', 0, 0)]
  transfers between devices with their start and end apart: 15 -> 0, of which waited for: 11 -> 0; matrix products, arithmetic and copies ran while one was open for 14% -> 0% of each run, Pallas kernels for 0% -> 0%
where the time goes in v2:
time: 301 us; the launch traced here: 298 us
  Pallas kernels  197 us (65%)
  matrix products  51.7 us (17%)
  local copies, waits for them, and re-layouts  31.3 us (10%)
  other arithmetic  15.9 us (5%)
    pallas_call x4, Pallas kernels, comm_call(): pl.pallas_call(body, out_shape=out_shape, in_specs=[VMEM] * len(args), ou...  197 us
    dot_general x14, matrix products, mm_nt(): lax.dot_general(a, b, (((1,), (1,)), ((), ())), preferred_element_type=F32)  21.3 us
    dot_general x14, matrix products, mm(): return jnp.dot(a, b, preferred_element_type=F32)  15.8 us
    dot_general x14, matrix products, mm_tn(): lax.dot_general(a, b, (((0,), (0,)), ((), ())), preferred_element_type=F32)  14.5 us
    unnamed x110, local copies, waits for them, and re-layouts  9.22 us

profile of v2, /device:TPU:0, one launch (start us, length us, event | category | flops | bytes accessed | tf_op | source)
XLA Modules:
  0.0 298.0 jit_solution(4461445190435216528)
XLA Ops:
  0.7 1.1 convert_element_type.284
  2.2 1.0 convert_element_type.285
  3.6 0.9 pad_maximum_fusion.3.wf
  7.1 1.6 multiply_bitcast_fusion
  9.4 53.5 %shard_map.263 = (bf16[1024,1024]{1,0:T(8,128)(2,1)}, bf16[1024,1024]{1,0:T(8,128)(2,1)}, bf16[8,4,32,640]{3,2,1,0:T(8,128)(2,1)}, bf16[8,32,704]{2,1,0:T(8,128)(2,1)}, bf16[4,32,1536]{2,1,0:T(8,128)(2,1)}) custom-call(bf16[128,1024]{1,0:T(8,128)(2,1)} %bitcast.123, bf16[128,1024]{1,0:T(8,128)(2,1)} %get-tuple-element.72.dy, ...), custom_call_target="tpu_custom_call" | custom-call | tf_op jit(solution)/shard_map/pallas_call | solution.py:450
  62.9 1.2 slice_convert_fusion
  65.0 2.1 fusion
  67.1 1.8 fusion.121
  71.3 0.9 fusion.122
  72.8 1.3 copy-done
  76.2 0.9 fusion.123
  77.8 1.4 copy-done.2
  80.8 2.1 convolution_convert_fusion.2.part
  83.6 46.9 %shard_map.264 = (f32[128,1024]{1,0:T(8,128)}, bf16[1024,1024]{1,0:T(8,128)(2,1)}, bf16[8,4,32,704]{3,2,1,0:T(8,128)(2,1)}, bf16[4,88,1024]{2,1,0:T(8,128)(2,1)}) custom-call(bf16[1024,1024]{1,0:T(8,128)(2,1)} %convolution_convert_fusion.2.part, bf16[128,1024]{1,0:T(8,128)(2,1)} %bitcast.124, f32[1,1024]{1,0:T(1,128)} %get-tuple-element.75.gain, ...), custom_call_target="tpu_custom_call" | custom-call | tf_op jit(solution)/shard_map/pallas_call | solution.py:450
  130.5 3.9 %fusion.124 = f32[1024,704]{0,1:T(8,128)S(1)} fusion(bf16[1024,1024]{1,0:T(8,128)(2,1)} %get-tuple-element.40, bf16[1024,704]{1,0:T(8,128)(2,1)} %bitcast.156), kind=kOutput, calls=%fused_computation.199 | convolution fusion | flops 1476395008 | bytes 6422528 | tf_op jit(solution)/shard_map/dot_general | solution.py:28
  134.4 1.5 multiply_convert_fusion.4
  136.0 1.8 convolution_convert_fusion.6
  137.8 0.8 copy-done.43
  138.6 2.8 convolution_convert_fusion.4
  141.4 2.6 copy.139
  144.0 5.0 %convolution_convert_fusion.3.part = bf16[1024,1024]{1,0:T(8,128)(2,1)} fusion(bf16[1024,704]{1,0:T(8,128)(2,1)} %bitcast.157, bf16[1024,352]{0,1:T(8,128)(2,1)} %copy-done.52, bf16[1024,352]{0,1:T(8,128)(2,1)} %copy-done.51), kind=kOutput, calls=%fused_computation.31 | convolution fusion | flops 1480327168 | bytes 4980736 | tf_op jit(solution)/shard_map/dot_general | solution.py:36
  149.0 46.0 %shard_map.265 = (f32[128,1024]{1,0:T(8,128)}, bf16[1024,1024]{1,0:T(8,128)(2,1)}, f32[1,1024]{1,0:T(1,128)}, bf16[8,32,704]{2,1,0:T(8,128)(2,1)}, f32[88,1024]{1,0:T(8,128)}) custom-call(bf16[1024,1024]{1,0:T(8,128)(2,1)} %convolution_convert_fusion.3.part, f32[128,1024]{1,0:T(8,128)} %get-tuple-element.71.gy, f32[128,1024]{1,0:T(8,128)} %get-tuple-element.42.hres, ...), custom_call_target="tpu_custom_call" | custom-call | tf_op jit(solution)/shard_map/pallas_call | solution.py:450
  195.0 2.6 convolution_convert_fusion.12
  198.0 2.2 multiply_convert_fusion
  202.6 1.1 multiply_convert_fusion.1
  203.7 0.8 fusion.26
  205.3 0.9 copy-done.6
  206.7 0.8 pad_maximum_fusion.4.gr
  209.8 1.6 fusion.25
  214.5 0.8 copy.148
  215.4 0.8 copy.149
  216.2 0.8 copy.150
  217.0 0.9 copy.151
  217.9 0.9 copy.152
  218.8 0.8 copy.153
  219.6 1.0 convolution_convert_fusion.15
  220.6 0.8 copy.147
  221.5 1.0 convolution_convert_fusion.16
  222.5 0.8 copy.146
  224.1 3.5 %concatenate.64 = bf16[1024,640]{1,0:T(8,128)(2,1)S(1)} concatenate(bf16[1024,64]{1,0:T(8,128)(2,1)} %copy.146, bf16[1024,64]{1,0:T(8,128)(2,1)} %copy.147, bf16[1024,32]{1,0:T(8,128)(2,1)} %copy.148, bf16[1024,32]{1,0:T(8,128)(2,1)} %copy.149, bf16[1024,32]{1,0:T(8,128)(2,1)} %copy.150, bf16[1024,32]{1,0:T(8,128)(2,1)} %copy.151, bf16[1024,32]{1,0:T(8,128)(2,1)} %copy.152, ...), dimensions={1} | concatenate | bytes 2621440 | tf_op jit(solution)/shard_map/concatenate | solution.py:949
  227.7 3.1 %convolution_convert_fusion.5 = bf16[1024,640]{1,0:T(8,128)(2,1)} fusion(bf16[1024,640]{1,0:T(8,128)(2,1)S(1)} %concatenate.64, bf16[1024,1024]{1,0:T(8,128)(2,1)S(1)} %copy-done.8, f32[1024]{0:T(1024)S(1)} %bitcast.155, f32[1024]{0:T(1024)S(1)} %copy-done.39), kind=kOutput, calls=%fused_computation.33 | convolution fusion | flops 1347026944 | bytes 4726784 | tf_op jit(solution)/shard_map/dot_general | solution.py:32
  230.8 2.7 convolution_convert_fusion.py
  233.5 3.1 %convolution_convert_fusion.1.part = bf16[1024,1024]{1,0:T(8,128)(2,1)} fusion(bf16[1024,640]{1,0:T(8,128)(2,1)S(1)} %concatenate.64, bf16[1024,640]{1,0:T(8,128)(2,1)S(1)} %bitcast.152), kind=kOutput, calls=%fused_computation.29 | convolution fusion | flops 1343225856 | bytes 4718592 | tf_op jit(solution)/shard_map/dot_general | solution.py:36
  236.6 50.2 %shard_map.266 = (f32[128,1024]{1,0:T(8,128)}, bf16[128,1024]{1,0:T(8,128)(2,1)}, f32[2,1024]{1,0:T(2,128)}, bf16[8,32,640]{2,1,0:T(8,128)(2,1)}, f32[32,1536]{1,0:T(8,128)}, /*index=5*/bf16[8,32,704]{2,1,0:T(8,128)(2,1)}) custom-call(bf16[1024,1024]{1,0:T(8,128)(2,1)} %convolution_convert_fusion.1.part, bf16[1024,1024]{1,0:T(8,128)(2,1)} %convolution_convert_fusion.py, ...), custom_call_target="tpu_custom_call" | custom-call | tf_op jit(solution)/shard_map/pallas_call | solution.py:450
  286.8 1.2 convert_bitcast_fusion
  288.3 0.9 reshape.237
  289.4 0.9 reshape.238
  296.2 0.8 copy.185
  (179 shorter events, 29.3 us)
Async XLA Ops:
  0.6 3.9 %copy-start.26 = (f32[32,1024]{1,0:T(8,128)S(1)}, f32[32,1024]{1,0:T(8,128)}, u32[]{:S(2)}) copy-start(f32[32,1024]{1,0:T(8,128)} %param.21) | copy-start | bytes 393220
  0.7 3.9 %copy-start.27 = (f32[32,1024]{1,0:T(8,128)S(1)}, f32[32,1024]{1,0:T(8,128)}, u32[]{:S(2)}) copy-start(f32[32,1024]{1,0:T(8,128)} %param.22) | copy-start | bytes 393220
  0.7 3.9 %copy-start.29 = (f32[32,512]{1,0:T(8,128)S(1)}, f32[32,512]{1,0:T(8,128)}, u32[]{:S(2)}) copy-start(f32[32,512]{1,0:T(8,128)} %param.23) | copy-start | bytes 196612
  0.7 4.0 %copy-start.46 = (f32[32]{0:T(128)S(1)}, f32[32]{0:T(128)}, u32[]{:S(2)}) copy-start(f32[32]{0:T(128)} %param.20) | copy-start | bytes 388
  0.7 4.1 %copy-start.47 = (f32[32]{0:T(128)S(1)}, f32[32]{0:T(128)}, u32[]{:S(2)}) copy-start(f32[32]{0:T(128)} %param.28) | copy-start | bytes 388
  0.7 4.2 %copy-start.35 = (f32[32,64]{1,0:T(8,128)S(1)}, f32[32,64]{1,0:T(8,128)}, u32[]{:S(2)}) copy-start(f32[32,64]{1,0:T(8,128)} %param.24) | copy-start | bytes 24580
  1.8 4.7 %copy-start.48 = (f32[8]{0:T(128)S(1)}, f32[8]{0:T(128)}, u32[]{:S(2)}) copy-start(f32[8]{0:T(128)} %param.19) | copy-start | bytes 100
  1.8 5.3 %copy-start.24 = (bf16[1,128,1024]{2,1,0:T(8,128)(2,1)S(1)}, bf16[1,128,1024]{2,1,0:T(8,128)(2,1)}, u32[]{:S(2)}) copy-start(bf16[1,128,1024]{2,1,0:T(8,128)(2,1)} %param.17) | copy-start | bytes 786436
  3.5 5.2 %copy-start.28 = (f32[32,1024]{1,0:T(8,128)S(1)}, f32[32,1024]{1,0:T(8,128)}, u32[]{:S(2)}) copy-start(f32[32,1024]{1,0:T(8,128)} %param.27) | copy-start | bytes 393220
  3.5 5.2 %copy-start.32 = (f32[32,256]{1,0:T(8,128)S(1)}, f32[32,256]{1,0:T(8,128)}, u32[]{:S(2)}) copy-start(f32[32,256]{1,0:T(8,128)} %param.25) | copy-start | bytes 98308
  3.6 5.2 %copy-start.33 = (f32[32,256]{1,0:T(8,128)S(1)}, f32[32,256]{1,0:T(8,128)}, u32[]{:S(2)}) copy-start(f32[32,256]{1,0:T(8,128)} %param.26) | copy-start | bytes 98308
  62.9 4.1 %copy-start.7 = (bf16[1024,1024]{1,0:T(8,128)(2,1)S(1)}, bf16[1024,1024]{1,0:T(8,128)(2,1)}, u32[]{:S(2)}) copy-start(bf16[1024,1024]{1,0:T(8,128)(2,1)} %get-tuple-element.34) | copy-start | bytes 6291460
  64.4 2.7 copy-start.30
  65.0 162.6 %copy-start.34 = (f32[1,1024]{1,0:T(1,128)}, f32[1,1024]{1,0:T(1,128)S(1)}, u32[]{:S(2)}) copy-start(f32[1,1024]{1,0:T(1,128)S(1)} %get-tuple-element.76.gain) | copy-start | bytes 12292
  67.1 1.8 copy-start.38
  68.9 8.9 %copy-start.4 = (bf16[1024,640]{0,1:T(8,128)(2,1)}, bf16[1024,640]{0,1:T(8,128)(2,1)S(1)}, u32[]{:S(2)}) copy-start(bf16[1024,640]{0,1:T(8,128)(2,1)S(1)} %get-tuple-element.87) | copy-start | bytes 3932164
  68.9 2.3 copy-start.40
  72.2 1.9 copy-start
  75.1 5.7 %copy-start.13 = (bf16[1024,64]{0,1:T(8,128)(2,1)}, bf16[1024,64]{0,1:T(8,128)(2,1)S(1)}, u32[]{:S(2)}) copy-start(bf16[1024,64]{0,1:T(8,128)(2,1)S(1)} %convolution_convert_fusion.13) | copy-start | bytes 393220
  77.1 2.0 copy-start.2
  80.6 2.3 copy-start.20
  80.8 2.1 copy-start.15
  130.5 3.9 %copy-start.42 = (bf16[1024,1024]{1,0:T(8,128)(2,1)S(1)}, bf16[1024,1024]{1,0:T(8,128)(2,1)}, u32[]{:S(2)}) copy-start(bf16[1024,1024]{1,0:T(8,128)(2,1)} %get-tuple-element.37) | copy-start | bytes 6291460
  130.5 3.9 %copy-start.44 = (bf16[4,88,1024]{2,1,0:T(8,128)(2,1)S(1)}, bf16[4,88,1024]{2,1,0:T(8,128)(2,1)}, u32[]{:S(2)}) copy-start(bf16[4,88,1024]{2,1,0:T(8,128)(2,1)} %get-tuple-element.39) | copy-start | bytes 2162692
  135.9 1.8 copy-start.49
  135.9 1.8 copy-start.51
  135.9 1.8 copy-start.52
  135.9 2.6 copy-start.43
  149.0 46.0 %copy-start.18 = (bf16[4,32,1536]{2,1,0:T(8,128)(2,1)S(1)}, bf16[4,32,1536]{2,1,0:T(8,128)(2,1)}, u32[]{:S(2)}) copy-start(bf16[4,32,1536]{2,1,0:T(8,128)(2,1)} %get-tuple-element.36) | copy-start | bytes 1179652
  195.0 2.9 copy-start.1
  198.0 2.2 copy-start.5
  200.2 2.4 copy-start.3
  204.4 2.3 copy-start.11
  204.4 1.8 copy-start.6
  204.4 1.8 copy-start.14
  204.5 1.8 copy-start.16
  213.9 5.7 %copy-start.10 = (bf16[1024,256]{1,0:T(8,128)(2,1)S(1)}, bf16[1024,256]{1,0:T(8,128)(2,1)}, u32[]{:S(2)}) copy-start(bf16[1024,256]{1,0:T(8,128)(2,1)} %copy-done.9) | copy-start | bytes 1572868
  213.9 7.6 %copy-start.12 = (bf16[1024,256]{1,0:T(8,128)(2,1)S(1)}, bf16[1024,256]{1,0:T(8,128)(2,1)}, u32[]{:S(2)}) copy-start(bf16[1024,256]{1,0:T(8,128)(2,1)} %copy-done.11) | copy-start | bytes 1572868
  224.1 3.5 %copy-start.8 = (bf16[1024,1024]{1,0:T(8,128)(2,1)S(1)}, bf16[1024,1024]{1,0:T(8,128)(2,1)}, u32[]{:S(2)}) copy-start(bf16[1024,1024]{1,0:T(8,128)(2,1)} %get-tuple-element.34) | copy-start | bytes 6291460
  224.1 3.5 %copy-start.39 = (f32[1024]{0:T(1024)S(1)}, f32[1024]{0:T(1024)}, u32[]{:S(2)}) copy-start(f32[1024]{0:T(1024)} %copy-done.38) | copy-start | bytes 12292
  227.6 3.1 %copy-start.45 = (bf16[4,88,1024]{2,1,0:T(8,128)(2,1)S(1)}, bf16[4,88,1024]{2,1,0:T(8,128)(2,1)}, u32[]{:S(2)}) copy-start(bf16[4,88,1024]{2,1,0:T(8,128)(2,1)} %get-tuple-element.39) | copy-start | bytes 2162692
  227.6 3.1 %copy-start.50 = (bf16[1024,352]{0,1:T(8,128)(2,1)S(1)}, bf16[1024,352]{0,1:T(8,128)(2,1)}, u32[]{:S(2)}) copy-start(bf16[1024,352]{0,1:T(8,128)(2,1)} %copy-done.49) | copy-start | bytes 2162692
  230.8 2.7 copy-start.31
  286.8 3.5 %copy-start.22 = (bf16[8,32,640]{2,1,0:T(8,128)(2,1)S(1)}, bf16[8,32,640]{2,1,0:T(8,128)(2,1)}, u32[]{:S(2)}) copy-start(bf16[8,32,640]{2,1,0:T(8,128)(2,1)} %get-tuple-element.50) | copy-start | bytes 983044
  288.0 4.3 %copy-start.25 = (f32[32,1536]{1,0:T(8,128)S(1)}, f32[32,1536]{1,0:T(8,128)}, u32[]{:S(2)}) copy-start(f32[32,1536]{1,0:T(8,128)} %get-tuple-element.51) | copy-start | bytes 589828
  288.3 7.2 %copy-start.23 = (bf16[128,1024]{1,0:T(8,128)(2,1)S(1)}, bf16[128,1024]{1,0:T(8,128)(2,1)}, u32[]{:S(2)}) copy-start(bf16[128,1024]{1,0:T(8,128)(2,1)} %get-tuple-element.47) | copy-start | bytes 786436
  289.2 7.1 %copy-start.19 = (f32[128,1024]{1,0:T(8,128)S(1)}, f32[128,1024]{1,0:T(8,128)}, u32[]{:S(2)}) copy-start(f32[128,1024]{1,0:T(8,128)} %get-tuple-element.48) | copy-start | bytes 1572868
  289.4 7.6 %copy-start.21 = (f32[88,1024]{1,0:T(8,128)S(1)}, f32[88,1024]{1,0:T(8,128)}, u32[]{:S(2)}) copy-start(f32[88,1024]{1,0:T(8,128)} %get-tuple-element.128) | copy-start | bytes 1081348
  (5 other events, 5.5 us)
